TPU v7x, 32 devices: a whole 2x2x4 slice. The times are simulated.
32 devices in a mesh: rep: 2 (over x), dp: 16 (over y, z, core).
Axes of the slice: x: 2, y: 2, z: 4, core: 2. Of those that a mesh axis runs over, the one named last changes fastest.
Arguments:
- g_w_gate: bfloat16 [32, 2, 1024, 3584], P(('rep', 'dp')), parts along dimension 0
- g_w_up: bfloat16 [32, 2, 1024, 3584], P(('rep', 'dp')), parts along dimension 0
- g_w_down: bfloat16 [32, 2, 3584, 1024], P(('rep', 'dp')), parts along dimension 0
- w_gate: bfloat16 [2, 1024, 3584], replicated
- w_up: bfloat16 [2, 1024, 3584], replicated
- w_down: bfloat16 [2, 3584, 1024], replicated
- m_w_gate: float32 [2, 1024, 3584], P(None, 'dp')
- m_w_up: float32 [2, 1024, 3584], P(None, 'dp')
- m_w_down: float32 [2, 3584, 1024], P(None, 'dp')
- v_w_gate: float32 [2, 1024, 3584], P(None, 'dp')
- v_w_up: float32 [2, 1024, 3584], P(None, 'dp')
- v_w_down: float32 [2, 3584, 1024], P(None, 'dp')
Outputs:
- output 1: bfloat16 [4, 1024, 3584], P('rep'), parts along dimension 0
- output 2: bfloat16 [4, 1024, 3584], P('rep'), parts along dimension 0
- output 3: bfloat16 [4, 3584, 1024], P('rep'), parts along dimension 0
- output 4: float32 [4, 1024, 3584], P('rep', 'dp'), parts along dimension 0
- output 5: float32 [4, 1024, 3584], P('rep', 'dp'), parts along dimension 0
- output 6: float32 [4, 3584, 1024], P('rep', 'dp'), parts along dimension 0
- output 7: float32 [4, 1024, 3584], P('rep', 'dp'), parts along dimension 0
- output 8: float32 [4, 1024, 3584], P('rep', 'dp'), parts along dimension 0
- output 9: float32 [4, 3584, 1024], P('rep', 'dp'), parts along dimension 0
There are 2 independent parts. A program takes and returns all parts, laid end to end along the dimension named above; an argument that names none is the same for every part.
All inputs are finite; a program needn't handle non-finite values.
Results may differ from a plain program's by a relative error of at most 0.022.
Values are sent between devices in bfloat16 or wider.
A program may use at most 2 GiB of HBM per device.

v0:
```python
import jax
import jax.numpy as jnp
from jax import lax
from jax.sharding import PartitionSpec as P


def adamw(w, m, v, g):
    m = 0.9 * m + 0.1 * g
    v = 0.95 * v + 0.05 * g * g
    step = m * lax.rsqrt(v + 1e-8) + 0.1 * w
    return (w - 0.02 * step).astype(jnp.bfloat16), m, v


def solution(mesh):
    def step(*arrays):
        terms, weights, m, v = (arrays[i : i + 3] for i in (0, 3, 6, 9))
        gradients = [lax.psum_scatter(t[0], "dp", scatter_dimension=1, tiled=True).astype(jnp.float32) for t in terms]
        me = lax.axis_index("dp")
        own = [lax.dynamic_slice_in_dim(w, me * one.shape[1], one.shape[1], 1).astype(jnp.float32) for w, one in zip(weights, m, strict=True)]
        new = [adamw(w, m, v, g) for w, m, v, g in zip(own, m, v, gradients, strict=True)]
        whole = [lax.all_gather(one[0], "dp", axis=1, tiled=True) for one in new]
        return (*whole, *(one[1] for one in new), *(one[2] for one in new))

    all_of, cut = P(None, None, None), P(None, "dp", None)
    return jax.shard_map(
        step,
        mesh=mesh,
        in_specs=(P(("rep", "dp"), None, None, None),) * 3 + (all_of,) * 3 + (cut,) * 6,
        out_specs=(P("rep", None, None),) * 3 + (P("rep", "dp", None),) * 6,
        check_vma=False,
    )
```

profile of v0, /device:TPU:0, one launch (start us, length us, event | category | flops | bytes accessed | tf_op | source)
XLA Modules:
  0.0 847.4 jit_solution(6367706756420278520)
XLA Ops:
  7.2 0.0 reduce-scatter.8.cloned.1.call-start
  7.2 0.7 reduce-scatter.8.cloned.1.call-update
  7.9 0.0 reduce-scatter.6.cloned.1.call-start
  8.0 0.7 reduce-scatter.6.cloned.1.call-update
  8.7 0.0 reduce-scatter.4.cloned.1.call-start
  8.7 0.0 copy-start.1
  8.7 0.7 reduce-scatter.4.cloned.1.call-update
  9.4 0.0 all-gather.8.cloned.1.call-start
  9.4 153.6 %reduce-scatter.8.cloned.1.call-done = bf16[2,224,1024]{2,1,0:T(8,128)(2,1)} async-done(((bf16[2,3584,1024]{2,1,0:T(8,128)(2,1)}), bf16[2,224,1024]{2,1,0:T(8,128)(2,1)}) %reduce-scatter.8.cloned.1.call-update) | async-done | bytes 917520 | tf_op jit(solution)/shard_map/reduce_scatter | solution.py:17
  163.0 0.0 copy-done.1
  163.0 4.8 fusion.10
  167.8 0.0 all-gather.8.cloned.1.call-update
  167.8 0.0 all-gather.6.cloned.1.call-start
  167.9 147.1 %reduce-scatter.6.cloned.1.call-done = bf16[2,64,3584]{2,1,0:T(8,128)(2,1)} async-done(((bf16[2,1024,3584]{2,1,0:T(8,128)(2,1)}), bf16[2,64,3584]{2,1,0:T(8,128)(2,1)}) %reduce-scatter.6.cloned.1.call-update) | async-done | bytes 917520 | tf_op jit(solution)/shard_map/reduce_scatter | solution.py:17
  315.0 0.0 copy-start.2
  315.0 5.4 fusion.6
  320.3 0.0 all-gather.6.cloned.1.call-update
  320.4 0.0 all-gather.4.cloned.1.call-start
  320.4 146.5 %reduce-scatter.4.cloned.1.call-done = bf16[2,64,3584]{2,1,0:T(8,128)(2,1)} async-done(((bf16[2,1024,3584]{2,1,0:T(8,128)(2,1)}), bf16[2,64,3584]{2,1,0:T(8,128)(2,1)}) %reduce-scatter.4.cloned.1.call-update) | async-done | bytes 917520 | tf_op jit(solution)/shard_map/reduce_scatter | solution.py:17
  466.9 0.0 copy-done.2
  466.9 4.7 fusion.2
  471.6 0.0 all-gather.4.cloned.1.call-update
  471.6 110.5 %all-gather.8.cloned.1.call-done = bf16[2,3584,1024]{2,1,0:T(8,128)(2,1)} async-done(((bf16[2,224,1024]{2,1,0:T(8,128)(2,1)}), bf16[2,3584,1024]{2,1,0:T(8,128)(2,1)}) %all-gather.8.cloned.1.call-update) | async-done | bytes 14680080 | tf_op jit(solution)/shard_map/all_gather | solution.py:21
  582.2 114.2 %all-gather.6.cloned.1.call-done = bf16[2,1024,3584]{2,1,0:T(8,128)(2,1)} async-done(((bf16[2,64,3584]{2,1,0:T(8,128)(2,1)}), bf16[2,1024,3584]{2,1,0:T(8,128)(2,1)}) %all-gather.6.cloned.1.call-update) | async-done | bytes 14680080 | tf_op jit(solution)/shard_map/all_gather | solution.py:21
  696.3 114.2 %all-gather.4.cloned.1.call-done = bf16[2,1024,3584]{2,1,0:T(8,128)(2,1)} async-done(((bf16[2,64,3584]{2,1,0:T(8,128)(2,1)}), bf16[2,1024,3584]{2,1,0:T(8,128)(2,1)}) %all-gather.4.cloned.1.call-update) | async-done | bytes 14680080 | tf_op jit(solution)/shard_map/all_gather | solution.py:21
  810.5 0.0 copy-start
  810.5 0.0 slice-start
  810.5 0.0 slice-start.1
  810.5 15.7 %copy.24 = bf16[2,1024,3584]{2,1,0:T(8,128)(2,1)} copy(bf16[2,1024,3584]{2,1,0:T(8,128)(2,1)} %all-gather.4.cloned.1.call-done) | data formatting | bytes 29360128
  826.2 0.0 copy-done
  826.2 0.0 slice-start.2
  826.2 0.0 slice-start.3
  826.3 7.4 copy.25
  833.7 0.0 slice-done
  833.7 0.0 slice-done.1
  833.7 0.1 slice-done.2
  833.8 1.3 slice-done.3
  835.1 5.5 copy.26
  (1 shorter events, 0.0 us)
Async XLA Ops:
  7.2 155.9 %reduce-scatter.8.cloned.1.call-start = ((), (), s32[]{:S(2)}) async-start(), calls=%async_computation.7 | async-start | bytes 15597568 | tf_op jit(solution)/shard_map/reduce_scatter | solution.py:17
  7.9 307.1 %reduce-scatter.6.cloned.1.call-start = ((), (), s32[]{:S(2)}) async-start(), calls=%async_computation.5 | async-start | bytes 15597568 | tf_op jit(solution)/shard_map/reduce_scatter | solution.py:17
  8.7 458.2 %reduce-scatter.4.cloned.1.call-start = ((), (), s32[]{:S(2)}) async-start(), calls=%async_computation.3 | async-start | bytes 15597568 | tf_op jit(solution)/shard_map/reduce_scatter | solution.py:17
  8.7 154.3 %copy-start.1 = (f32[2,224,1024]{2,1,0:T(8,128)S(1)}, f32[2,224,1024]{2,1,0:T(8,128)}, u32[]{:S(2)}) copy-start(f32[2,224,1024]{2,1,0:T(8,128)} %param.23) | copy-start | bytes 5505028
  9.4 572.8 %all-gather.8.cloned.1.call-start = ((), (), s32[]{:S(2)}) async-start(), calls=%async_computation.8 | async-start | bytes 15597568 | tf_op jit(solution)/shard_map/all_gather | solution.py:21
  167.8 528.5 %all-gather.6.cloned.1.call-start = ((), (), s32[]{:S(2)}) async-start(), calls=%async_computation.6 | async-start | bytes 15597568 | tf_op jit(solution)/shard_map/all_gather | solution.py:21
  315.0 151.9 %copy-start.2 = (f32[2,64,3584]{2,1,0:T(8,128)S(1)}, f32[2,64,3584]{2,1,0:T(8,128)}, u32[]{:S(2)}) copy-start(f32[2,64,3584]{2,1,0:T(8,128)} %param.21) | copy-start | bytes 5505028
  320.4 490.2 %all-gather.4.cloned.1.call-start = ((), (), s32[]{:S(2)}) async-start(), calls=%async_computation.4 | async-start | bytes 15597568 | tf_op jit(solution)/shard_map/all_gather | solution.py:21
  810.5 15.7 %copy-start = (bf16[2,1024,3584]{2,1,0:T(8,128)(2,1)S(1)}, bf16[2,1024,3584]{2,1,0:T(8,128)(2,1)}, u32[]{:S(2)}) copy-start(bf16[2,1024,3584]{2,1,0:T(8,128)(2,1)} %all-gather.6.cloned.1.call-done) | copy-start | bytes 44040196
  810.5 23.2 %slice-start = ((s8[14680064]{0:T(1024)(128)(4,1)}), s8[4194304]{0:T(1024)(128)(4,1)S(1)}, s32[]{:S(2)}) async-start(s8[14680064]{0:T(1024)(128)(4,1)} %bitcast.6), calls=%async_computation.9 | async-start | bytes 8388608
  810.5 23.2 %slice-start.1 = ((s8[14680064]{0:T(1024)(128)(4,1)}), s8[4194304]{0:T(1024)(128)(4,1)S(1)}, s32[]{:S(2)}) async-start(s8[14680064]{0:T(1024)(128)(4,1)} %bitcast.6), calls=%async_computation.10 | async-start | bytes 8388608
  826.2 7.6 slice-start.2
  826.2 8.9 %slice-start.3 = ((s8[14680064]{0:T(1024)(128)(4,1)}), s8[2097152]{0:T(1024)(128)(4,1)S(1)}, s32[]{:S(2)}) async-start(s8[14680064]{0:T(1024)(128)(4,1)} %bitcast.6), calls=%async_computation.12 | async-start | bytes 4194304
Sparse Core Ops, SparseCore 0:
  12.0 150.9 reduce-scatter.7
  167.1 147.8 reduce-scatter.5
  319.0 147.8 reduce-scatter.3
  469.6 112.5 all-gather.7
  584.8 111.4 all-gather.5
  699.0 111.4 all-gather.3
where the time goes:
time: 848 us; the launch traced here: 847 us
  waiting for transfers between devices  788 us (93%)
  local copies, waits for them, and re-layouts  30.1 us (4%)
  other arithmetic  14.8 us (2%)
  between operations  14.1 us (2%)
    reduce_scatter x3, waiting for transfers between devices, step(): lax.psum_scatter(t[0], 'dp', scatter_dimension=1, tiled=True)  447 us
    all_gather x3, waiting for transfers between devices, step(): whole = [lax.all_gather(one[0], 'dp', axis=1, tiled=True) for one in new]  339 us
    unnamed x17, local copies, waits for them, and re-layouts  30.1 us
  transfers between devices with their start and end apart: 6, of which 6 were waited for; matrix products, arithmetic and copies ran while one was open for 2% of the time, Pallas kernels for 0%

commit v1 on v0

v1 whole, which is shorter than its diff:
```python
import functools

import jax
import jax.numpy as jnp
from jax import lax
from jax.experimental import pallas as pl
from jax.experimental.pallas import tpu as pltpu
from jax.sharding import PartitionSpec as P

MESH = pl.DeviceIdType.MESH
ANY = pl.BlockSpec(memory_space=pl.ANY)
ROUNDS = 8
SLOTS = 4
LOADS = 2
NAMES = ("gate", "up", "down")
TYPES = (("y",) * 8, ("z",) * 8, ("y", "y", "y", "z") * 2)
LAGS = {
    "y": (("fetch", 0), ("moments", 4), ("first", 3), ("near", 4), ("far", 5), ("step", 6), ("pass1", 7), ("pass2", 8), ("pass3", 9)),
    "z": (("fetch", 0), ("moments", 5), ("first", 3), ("near", 4), ("far", 5), ("cross", 6), ("step", 7), ("pass0", 8), ("pass1", 9), ("pass2", 10)),
}
ORDER = ("fetch", "moments", "first", "near", "far", "cross", "step", "pass0", "pass1", "pass2", "pass3")
KEYS = ("s", "d", "rb", "wb", "gb", "wl", "ml", "vl", "ld", "dr", "ds", "ss", "rr", "ar", "ad", "ay", "az", "lo", "adr", "mo", "free")


def new_moments(m, v, g):
    return 0.9 * m + 0.1 * g, 0.95 * v + 0.05 * g * g


def new_weight(w, m, v):
    return (w - 0.02 * (m * lax.rsqrt(v + 1e-8) + 0.1 * w)).astype(jnp.bfloat16)


def piece(which, r):
    layer, q = r // 4, lax.rem(r, 4)
    if which == 2:
        return layer, pl.ds(pl.multiple_of(q // 2 * 112, 112), 112), pl.ds(pl.multiple_of(lax.rem(q, 2) * 512, 512), 512)
    return layer, pl.ds(pl.multiple_of(q * 16, 16), 16), pl.ds(0, 3584)


def shape_of(which):
    return (112, 512) if which == 2 else (16, 3584)


def scratch(which):
    rows, cols = shape_of(which)
    bf, f32, dma = jnp.bfloat16, jnp.float32, pltpu.SemaphoreType.DMA
    return (
        pltpu.VMEM((SLOTS, 8, rows, cols), bf),
        pltpu.VMEM((SLOTS, 8, rows, cols), bf),
        pltpu.VMEM((ROUNDS, 9 if which == 0 else 11, rows, cols), bf),
        pltpu.VMEM((ROUNDS, rows, cols), bf),
        pltpu.VMEM((ROUNDS, rows, cols), bf),
        pltpu.VMEM((LOADS, rows, cols), bf),
        pltpu.VMEM((LOADS, rows, cols), f32),
        pltpu.VMEM((LOADS, rows, cols), f32),
        dma((SLOTS,)),
        dma((SLOTS,)),
        dma,
        dma((SLOTS,)),
        dma((ROUNDS, 11)),
        dma((ROUNDS, 8)),
        dma,
        dma((2,)),
        dma((2,)),
        dma,
        dma,
        dma((LOADS, 3)),
        pltpu.SemaphoreType.REGULAR,
    )


class Weight:
    pass


def kernel(*refs):
    rep, me = lax.axis_index("rep"), lax.axis_index("dp")
    y, z, c = me // 8, lax.rem(me // 2, 4), lax.rem(me, 2)
    own = me // 2
    partner, across = me + 1 - 2 * c, me + 8 - 16 * y
    mid = (z > 0) & (z < 3)
    corner = (z == 0) | (z == 3)
    low = 1 - z // 2
    odd = lax.rem(z, 2)
    onward = me + 4 * low - 2
    e = (3 * low, 1 + low, low * (1 - z) + (1 - low) * (5 - z))
    e_to = (onward, onward, me + 2 - 4 * odd)
    e_slot = (e[0], e[1] + z // 2 * (1 - odd) * (4 - e[1]), e[2] + odd * (4 - e[2]))
    f = (z + 1 - 2 * odd, 2 - z // 2, 3 * low)
    f_to = (onward, me + 2 - 4 * low, me + 2 - 4 * low)

    inputs, outputs, rest = refs[:12], refs[12:18], refs[18:]
    weights = []
    for i in range(3):
        x = Weight()
        x.which, x.types = i, TYPES[i]
        x.g, x.w, x.m, x.v = inputs[i], inputs[3 + i], inputs[6 + i], inputs[9 + i]
        x.out, x.gout = outputs[i], outputs[3 + i]
        for key, ref in zip(KEYS, rest[i * len(KEYS) : (i + 1) * len(KEYS)], strict=True):
            setattr(x, key, ref)
        weights.append(x)

    def send(src, dst, sent, got, to):
        return pltpu.make_async_remote_copy(src_ref=src, dst_ref=dst, send_sem=sent, recv_sem=got, device_id=(rep, to), device_id_type=MESH)

    def arrive(ref, sem):
        send(ref, ref, sem, sem, partner).wait_recv()

    def left(ref, sem):
        send(ref, ref, sem, sem, partner).wait_send()

    def blocks(x, ref, r, j, core):
        layer, rows, cols = piece(x.which, r)
        return ref.at[layer, j, core, rows, cols]

    def mine(x, ref, r):
        layer, rows, cols = piece(x.which, r)
        return ref.at[layer, rows, cols]

    def add(x, dst, *terms):
        def slab(k, carry):
            rows = pl.ds(pl.multiple_of(k * 16, 16), 16)
            total = terms[0][rows, :].astype(jnp.float32)
            for term in terms[1:]:
                total += term[rows, :].astype(jnp.float32)
            dst[rows, :] = total.astype(jnp.bfloat16)
            return carry

        lax.fori_loop(0, shape_of(x.which)[0] // 16, slab, 0)

    def ends(x, r, base):
        def when(then):
            @pl.when(mid)
            def _():
                arrive(x.rb.at[r, base + z], x.rr.at[r, base + z])
                arrive(x.rb.at[r, base + 4], x.rr.at[r, base + 4])
                then(x.rb.at[r, base + z], x.rb.at[r, base + 4])

            @pl.when(corner)
            def _():
                at = base + 4 - z // 3
                arrive(x.rb.at[r, at], x.rr.at[r, at])
                then(x.rb.at[r, at])

        return when

    def fetch(x, kind, r):
        slot = lax.rem(r, SLOTS)

        @pl.when(r >= SLOTS)
        def _():
            left(x.s.at[slot, pl.ds(0, 7)], x.ss.at[slot])
            pl.semaphore_wait(x.free, 1)

        pltpu.make_async_copy(blocks(x, x.g, r, slice(None), c), x.s.at[slot], x.ld.at[slot]).start()
        send(blocks(x, x.g, r, slice(None), 1 - c), x.d.at[slot], x.ds, x.dr.at[slot], partner).start()

    def moments(x, kind, r):
        slot = lax.rem(r, LOADS)
        layer, rows, cols = piece(x.which, r)
        pltpu.make_async_copy(x.w.at[layer, own, c, rows, cols], x.wl.at[slot], x.mo.at[slot, 0]).start()
        pltpu.make_async_copy(mine(x, x.m, r), x.ml.at[slot], x.mo.at[slot, 1]).start()
        pltpu.make_async_copy(mine(x, x.v, r), x.vl.at[slot], x.mo.at[slot, 2]).start()

    def along(x, r, slot, row, k, base, *terms):
        j = row * 4 + e[k]
        to = base + e_slot[k]
        send(x.s.at[slot, j], x.rb.at[r, to], x.ss.at[slot], x.rr.at[r, to], e_to[k]).start()

    def first(x, kind, r):
        slot = lax.rem(r, SLOTS)
        pltpu.make_async_copy(blocks(x, x.g, r, slice(None), c), x.s.at[slot], x.ld.at[slot]).wait()
        arrive(x.d.at[slot], x.dr.at[slot])
        if kind == "y":
            for col in (*e, z):
                j = (1 - y) * 4 + col
                add(x, x.s.at[slot, j], x.s.at[slot, j], x.d.at[slot, j])
                send(x.s.at[slot, j], x.rb.at[r, col], x.ss.at[slot], x.rr.at[r, col], across).start()
        else:

            @pl.when(corner)
            def _():
                for row in (1 - y, y):
                    for k in range(3):
                        j = row * 4 + e[k]
                        add(x, x.s.at[slot, j], x.s.at[slot, j], x.d.at[slot, j])
                        along(x, r, slot, row, k, row * 5)

    def hops(x, kind, r, ks):
        slot = lax.rem(r, SLOTS)
        if kind == "y":
            for k in ks:
                j = y * 4 + e[k]
                arrive(x.rb.at[r, e[k]], x.rr.at[r, e[k]])

                @pl.when(mid)
                def _():
                    arrive(x.rb.at[r, 4 + e[k]], x.rr.at[r, 4 + e[k]])
                    add(x, x.s.at[slot, j], x.s.at[slot, j], x.d.at[slot, j], x.rb.at[r, e[k]], x.rb.at[r, 4 + e[k]])

                @pl.when(corner)
                def _():
                    add(x, x.s.at[slot, j], x.s.at[slot, j], x.d.at[slot, j], x.rb.at[r, e[k]])

                along(x, r, slot, y, k, 4)
        else:

            @pl.when(mid)
            def _():
                for row in (1 - y, y):
                    for k in ks:
                        j = row * 4 + e[k]
                        at = row * 5 + e[k]
                        arrive(x.rb.at[r, at], x.rr.at[r, at])
                        add(x, x.s.at[slot, j], x.s.at[slot, j], x.d.at[slot, j], x.rb.at[r, at])
                        along(x, r, slot, row, k, row * 5)

    def near(x, kind, r):
        hops(x, kind, r, (0, 1))

    def far(x, kind, r):
        hops(x, kind, r, (2,))

    def cross(x, kind, r):
        slot = lax.rem(r, SLOTS)
        j = (1 - y) * 4 + z
        ends(x, r, (1 - y) * 5)(lambda *got: add(x, x.s.at[slot, j], x.s.at[slot, j], x.d.at[slot, j], *got))
        send(x.s.at[slot, j], x.rb.at[r, 10], x.ss.at[slot], x.rr.at[r, 10], across).start()

    def share(x, kind, r, src, j, to_y, to_z):
        dst = blocks(x, x.out, r, j, c)
        t = 0 if kind == "y" else 1
        if to_y:
            send(src, dst, x.ay.at[t], x.ar.at[r, j], across).start()
        if to_z:

            @pl.when(z < 3)
            def _():
                send(src, dst, x.az.at[t], x.ar.at[r, j], me + 2).start()

            @pl.when(z > 0)
            def _():
                send(src, dst, x.az.at[t], x.ar.at[r, j], me - 2).start()

        send(src, dst, x.ad, x.adr, partner).start()

    def step(x, kind, r):
        slot, at = lax.rem(r, SLOTS), lax.rem(r, LOADS)
        over = z if kind == "y" else 10
        arrive(x.rb.at[r, over], x.rr.at[r, over])
        base = 4 if kind == "y" else y * 5
        ends(x, r, base)(lambda *got: add(x, x.gb.at[r], x.s.at[slot, own], x.d.at[slot, own], x.rb.at[r, over], *got))
        layer, rows, cols = piece(x.which, r)
        pltpu.make_async_copy(x.w.at[layer, own, c, rows, cols], x.wl.at[at], x.mo.at[at, 0]).wait()
        pltpu.make_async_copy(mine(x, x.m, r), x.ml.at[at], x.mo.at[at, 1]).wait()
        pltpu.make_async_copy(mine(x, x.v, r), x.vl.at[at], x.mo.at[at, 2]).wait()

        def slab(k, carry):
            rows = pl.ds(pl.multiple_of(k * 16, 16), 16)
            m, v = new_moments(x.ml[at, rows, :], x.vl[at, rows, :], x.gb[r, rows, :].astype(jnp.float32))
            x.wb[r, rows, :] = new_weight(x.wl[at, rows, :].astype(jnp.float32), m, v)
            return carry

        lax.fori_loop(0, shape_of(x.which)[0] // 16, slab, 0)
        share(x, kind, r, x.wb.at[r], own, True, True)
        pltpu.make_async_copy(x.wb.at[r], blocks(x, x.out, r, own, c), x.lo).start()
        pltpu.make_async_copy(x.gb.at[r], mine(x, x.gout, r), x.lo).start()

        @pl.when(r < ROUNDS - SLOTS)
        def _():
            pl.semaphore_signal(x.free, inc=1, device_id=(rep, partner), device_id_type=MESH)

    def came(x, r, j):
        arrive(blocks(x, x.out, r, j, c), x.ar.at[r, j])
        return blocks(x, x.out, r, j, c)

    def pass0(x, kind, r):
        j = (1 - y) * 4 + z
        share(x, kind, r, came(x, r, j), j, False, True)

    def passes(x, kind, r, ks):
        t = 0 if kind == "y" else 1
        for row in (y,) if kind == "y" else (y, 1 - y):
            for k in ks:
                j = row * 4 + f[k]
                src = came(x, r, j)

                @pl.when(mid)
                def _():
                    send(src, src, x.az.at[t], x.ar.at[r, j], f_to[k]).start()

                share(x, kind, r, src, j, kind == "y", False)

    def pass1(x, kind, r):
        passes(x, kind, r, (0, 1))

    def pass2(x, kind, r):
        passes(x, kind, r, (2,))

    def pass3(x, kind, r):
        for col in (z, *f):
            j = (1 - y) * 4 + col
            share(x, kind, r, came(x, r, j), j, False, False)

    stages = {one.__name__: one for one in (fetch, moments, first, near, far, cross, step, pass0, pass1, pass2, pass3)}

    barrier = pltpu.get_barrier_semaphore()
    pl.semaphore_signal(barrier, inc=1, device_id=(rep, partner), device_id_type=MESH)
    pl.semaphore_signal(barrier, inc=1, device_id=(rep, across), device_id_type=MESH)

    @pl.when(z < 3)
    def _():
        pl.semaphore_signal(barrier, inc=1, device_id=(rep, me + 2), device_id_type=MESH)

    @pl.when(z > 0)
    def _():
        pl.semaphore_signal(barrier, inc=1, device_id=(rep, me - 2), device_id_type=MESH)

    @pl.when(mid)
    def _():
        pl.semaphore_wait(barrier, 4)

    @pl.when(corner)
    def _():
        pl.semaphore_wait(barrier, 3)

    def turn(i, carry):
        for sub in range(3):
            for name in ORDER:
                for kind in ("y", "z"):
                    lag = dict(LAGS[kind]).get(name)
                    if lag is None:
                        continue
                    x = weights[(sub - lag) % 3]
                    if kind not in x.types:
                        continue
                    r = i + (sub - lag) // 3
                    ok = (r >= 0) & (r < ROUNDS)
                    if len(set(x.types)) > 1:
                        last = lax.rem(r + 4, 4) == 3
                        ok = ok & (last if kind == "z" else jnp.logical_not(last))
                    pl.when(ok)(functools.partial(stages[name], x, kind, r))
        return carry

    longest = max(lag for kind in LAGS.values() for _, lag in kind)
    lax.fori_loop(0, ROUNDS + (longest + 2) // 3, turn, 0)

    for x in weights:
        for slot in range(SLOTS):
            left(x.s.at[slot, pl.ds(0, 7)], x.ss.at[slot])
        for t, kind in enumerate(("y", "z")):
            n = x.types.count(kind)
            if n:
                left(x.rb.at[pl.ds(0, n), pl.ds(0, 4 if kind == "y" else 1)], x.ay.at[t])

                @pl.when(mid)
                def _():
                    if kind == "y":
                        left(x.rb.at[pl.ds(0, n), pl.ds(0, 5)], x.az.at[t])
                    else:
                        left(x.rb.at[pl.ds(0, n), pl.ds(0, 10)], x.az.at[t])

                @pl.when(corner)
                def _():
                    left(x.rb.at[pl.ds(0, n), pl.ds(0, 1 if kind == "y" else 2)], x.az.at[t])

        left(x.rb.at[:, pl.ds(0, 8)], x.ds)
        left(x.rb.at[:, pl.ds(0, 8)], x.ad)
        arrive(x.rb.at[:, pl.ds(0, 8)], x.adr)
        arrive(x.rb.at[:, pl.ds(0, 2)], x.lo)


def solution(mesh):
    def step(*arrays):
        terms, weights, m, v = (arrays[i : i + 3] for i in (0, 3, 6, 9))

        def cut(one):
            rows, cols = one.shape[-2:]
            return one.reshape(2, 8, 2, rows // 16, cols)

        wide = [cut(one) for one in weights]
        outs = pl.pallas_call(
            kernel,
            out_shape=[jax.ShapeDtypeStruct(one.shape, jnp.bfloat16) for one in (*wide, *m)],
            in_specs=[ANY] * 12,
            out_specs=[ANY] * 6,
            scratch_shapes=[one for i in range(3) for one in scratch(i)],
            compiler_params=pltpu.CompilerParams(collective_id=0, has_side_effects=True, vmem_limit_bytes=67043328),
            name="sum_step_gather",
        )(*(cut(t[0]) for t in terms), *wide, *m, *v)
        whole = [one.reshape(w.shape) for one, w in zip(outs[:3], weights, strict=True)]
        new = [new_moments(*mvg) for mvg in zip(m, v, (g.astype(jnp.float32) for g in outs[3:]), strict=True)]
        return (*whole, *(one[0] for one in new), *(one[1] for one in new))

    all_of, cut = P(None, None, None), P(None, "dp", None)
    return jax.shard_map(
        step,
        mesh=mesh,
        in_specs=(P(("rep", "dp"), None, None, None),) * 3 + (all_of,) * 3 + (cut,) * 6,
        out_specs=(P("rep", None, None),) * 3 + (P("rep", "dp", None),) * 6,
        check_vma=False,
    )
```

time: 848 us -> 514 us (0.61)
  waiting for transfers between devices: 788 us -> 0 us
  Pallas kernels: 0 us -> 476 us
  between operations: 14.1 us -> 0.71 us
    pallas_call x0 -> x1, Pallas kernels: none -> 476 us  [step(): pl.pallas_call(kernel, out_shape=[jax.ShapeDtypeStruct(one.shape, jnp.bfl...]
    reduce_scatter x3 -> x0, waiting for transfers between devices: 447 us -> none  [step(): lax.psum_scatter(t[0], 'dp', scatter_dimension=1, tiled=True)]
    all_gather x3 -> x0, waiting for transfers between devices: 339 us -> none  [step(): whole = [lax.all_gather(one[0], 'dp', axis=1, tiled=True) for one in new]]
    convert_element_type x3 -> x0, other arithmetic: 14.8 us -> none  [adamw(): return ((w - 0.02 * step).astype(jnp.bfloat16), m, v)]
    add x0 -> x2, other arithmetic: none -> 13.8 us  [new_moments(): return (0.9 * m + 0.1 * g, 0.95 * v + 0.05 * g * g)]
    unnamed x17 -> x21, local copies, waits for them, and re-layouts: 30.1 us -> 23.9 us
  transfers between devices with their start and end apart: 6 -> 0, of which waited for: 6 -> 0; matrix products, arithmetic and copies ran while one was open for 2% -> 0% of each run, Pallas kernels for 0% -> 0%
where the time goes in v1:
time: 514 us
  Pallas kernels  476 us (93%)
  local copies, waits for them, and re-layouts  23.9 us (5%)
  other arithmetic  13.8 us (3%)
    pallas_call x1, Pallas kernels, step(): pl.pallas_call(kernel, out_shape=[jax.ShapeDtypeStruct(one.shape, jnp.bfl...  476 us
    unnamed x21, local copies, waits for them, and re-layouts  23.9 us
    add x2, other arithmetic, new_moments(): return (0.9 * m + 0.1 * g, 0.95 * v + 0.05 * g * g)  13.8 us

profile of v1, /device:TPU:0, one launch (start us, length us, event | category | flops | bytes accessed | tf_op | source)
XLA Modules:
  0.0 514.0 jit_solution(1919843851470407233)
XLA Ops:
  0.6 475.6 %sum_step_gather.1 = (bf16[2,8,2,64,3584]{4,3,2,1,0:T(8,128)(2,1)}, bf16[2,8,2,64,3584]{4,3,2,1,0:T(8,128)(2,1)}, bf16[2,8,2,224,1024]{4,3,2,1,0:T(8,128)(2,1)},...) custom-call(bf16[2,8,2,64,3584]{4,3,2,1,0:T(8,128)(2,1)} %bitcast.16, ...), custom_call_target="tpu_custom_call" | custom-call | tf_op jit(solution)/shard_map/sum_step_gather/pallas_call | solution.py:382
  476.2 0.0 copy-start
  476.2 0.0 slice-start.4
  476.2 0.0 slice-start.5
  476.2 7.9 %fusion.3 = (f32[2,64,3584]{2,1,0:T(8,128)}, f32[2,64,3584]{2,1,0:T(8,128)}, f32[2,64,3584]{2,1,0:T(8,128)}, f32[2,64,3584]{2,1,0:T(8,128)}) fusion(bf16[2,64,3584]{2,1,0:T(8,128)(2,1)} %get-tuple-element.18, f32[2,64,3584]{2,1,0:T(8,128)} %refs_9_.1, f32[2,64,3584]{2,1,0:T(8,128)} %refs_6_.1, bf16[2,64,3584]{2,1,0:T(8,128)(2,1)} %get-tuple-element.19, ...), kind=kLoop, calls=%fused_computation.9 | loop fusion | flops 7340032 | bytes 16515072 | tf_op jit(solution)/shard_map/add | solution.py:26
  484.1 5.9 %fusion.5 = (f32[2,224,1024]{2,1,0:T(8,128)}, f32[2,224,1024]{2,1,0:T(8,128)}) fusion(bf16[2,224,1024]{2,1,0:T(8,128)(2,1)} %get-tuple-element.20, f32[2,224,1024]{2,1,0:T(8,128)} %refs_11_.1, f32[2,224,1024]{2,1,0:T(8,128)} %refs_8_.1), kind=kLoop, calls=%fused_computation.11 | loop fusion | flops 3670016 | bytes 8257536 | tf_op jit(solution)/shard_map/add | solution.py:26
  490.1 0.0 copy-done
  490.1 0.0 slice-start.6
  490.1 0.0 slice-start.7
  490.1 0.0 slice-start
  490.1 0.0 slice-start.1
  490.1 7.4 %copy.24 = bf16[2,1024,3584]{2,1,0:T(8,128)(2,1)} copy(bf16[2,1024,3584]{2,1,0:T(8,128)(2,1)S(1)} %bitcast.15) | data formatting | bytes 29360128
  497.6 0.0 slice-done.4
  497.6 0.0 slice-done.5
  497.6 0.0 slice-done.6
  497.6 1.5 slice-done.7
  499.1 0.0 slice-start.2
  499.1 0.0 slice-start.3
  499.1 7.4 %copy.25 = bf16[2,1024,3584]{2,1,0:T(8,128)(2,1)} copy(bf16[2,1024,3584]{2,1,0:T(8,128)(2,1)S(1)} %bitcast.14) | data formatting | bytes 29360128
  506.5 0.0 slice-done
  506.5 0.0 slice-done.1
  506.5 1.4 slice-done.2
  508.0 0.6 slice-done.3
  508.6 5.5 %copy.26 = bf16[2,3584,1024]{2,1,0:T(8,128)(2,1)} copy(bf16[2,3584,1024]{2,1,0:T(8,128)(2,1)S(1)} %bitcast.11) | data formatting | bytes 29360128
  (2 shorter events, 0.0 us)
Async XLA Ops:
  476.2 13.9 %copy-start = (bf16[2,8,2,64,3584]{4,3,2,1,0:T(8,128)(2,1)S(1)}, bf16[2,8,2,64,3584]{4,3,2,1,0:T(8,128)(2,1)}, u32[]{:S(2)}) copy-start(bf16[2,8,2,64,3584]{4,3,2,1,0:T(8,128)(2,1)} %get-tuple-element.15) | copy-start | bytes 44040196
  476.2 21.3 %slice-start.4 = ((s8[14680064]{0:T(1024)(128)(4,1)}), s8[2097152]{0:T(1024)(128)(4,1)S(1)}, s32[]{:S(2)}) async-start(s8[14680064]{0:T(1024)(128)(4,1)} %bitcast.12), calls=%async_computation.4 | async-start | bytes 4194304
  476.2 21.3 %slice-start.5 = ((s8[14680064]{0:T(1024)(128)(4,1)}), s8[4194304]{0:T(1024)(128)(4,1)S(1)}, s32[]{:S(2)}) async-start(s8[14680064]{0:T(1024)(128)(4,1)} %bitcast.12), calls=%async_computation.5 | async-start | bytes 8388608
  490.1 7.5 %slice-start.6 = ((s8[14680064]{0:T(1024)(128)(4,1)}), s8[4194304]{0:T(1024)(128)(4,1)S(1)}, s32[]{:S(2)}) async-start(s8[14680064]{0:T(1024)(128)(4,1)} %bitcast.12), calls=%async_computation.6 | async-start | bytes 8388608
  490.1 9.0 %slice-start.7 = ((s8[14680064]{0:T(1024)(128)(4,1)}), s8[4194304]{0:T(1024)(128)(4,1)S(1)}, s32[]{:S(2)}) async-start(s8[14680064]{0:T(1024)(128)(4,1)} %bitcast.12), calls=%async_computation.7 | async-start | bytes 8388608
  490.1 16.4 %slice-start = ((s8[14680064]{0:T(1024)(128)(4,1)}), s8[4194304]{0:T(1024)(128)(4,1)S(1)}, s32[]{:S(2)}) async-start(s8[14680064]{0:T(1024)(128)(4,1)} %bitcast.9), calls=%async_computation | async-start | bytes 8388608
  490.1 16.4 %slice-start.1 = ((s8[14680064]{0:T(1024)(128)(4,1)}), s8[4194304]{0:T(1024)(128)(4,1)S(1)}, s32[]{:S(2)}) async-start(s8[14680064]{0:T(1024)(128)(4,1)} %bitcast.9), calls=%async_computation.1 | async-start | bytes 8388608
  499.1 8.9 %slice-start.2 = ((s8[14680064]{0:T(1024)(128)(4,1)}), s8[4194304]{0:T(1024)(128)(4,1)S(1)}, s32[]{:S(2)}) async-start(s8[14680064]{0:T(1024)(128)(4,1)} %bitcast.9), calls=%async_computation.2 | async-start | bytes 8388608
  499.1 9.5 %slice-start.3 = ((s8[14680064]{0:T(1024)(128)(4,1)}), s8[2097152]{0:T(1024)(128)(4,1)S(1)}, s32[]{:S(2)}) async-start(s8[14680064]{0:T(1024)(128)(4,1)} %bitcast.9), calls=%async_computation.3 | async-start | bytes 4194304

commit v2 on v1

--- a/solution.py
+++ b/solution.py
@@ -9,17 +9,17 @@
 
 MESH = pl.DeviceIdType.MESH
 ANY = pl.BlockSpec(memory_space=pl.ANY)
-ROUNDS = 8
+ROUNDS = 16
 SLOTS = 4
 LOADS = 2
 NAMES = ("gate", "up", "down")
-TYPES = (("y",) * 8, ("z",) * 8, ("y", "y", "y", "z") * 2)
+TYPES = (("y",) * ROUNDS, ("z",) * ROUNDS, ("y", "y", "y", "z") * (ROUNDS // 4))
 LAGS = {
-    "y": (("fetch", 0), ("moments", 4), ("first", 3), ("near", 4), ("far", 5), ("step", 6), ("pass1", 7), ("pass2", 8), ("pass3", 9)),
-    "z": (("fetch", 0), ("moments", 5), ("first", 3), ("near", 4), ("far", 5), ("cross", 6), ("step", 7), ("pass0", 8), ("pass1", 9), ("pass2", 10)),
+    "y": {"fetch": 0, "first": 3, "outer": 4, "inner": 5, "last": 6, "moments": 5, "step": 7, "hop1": 8, "hop2": 9, "hop3": 10, "over": 11},
+    "z": {"fetch": 0, "outer": 3, "inner": 4, "last": 5, "cross": 6, "moments": 5, "step": 7, "pass0": 8, "hop1": 9, "hop2": 10, "hop3": 11},
 }
-ORDER = ("fetch", "moments", "first", "near", "far", "cross", "step", "pass0", "pass1", "pass2", "pass3")
-KEYS = ("s", "d", "rb", "wb", "gb", "wl", "ml", "vl", "ld", "dr", "ds", "ss", "rr", "ar", "ad", "ay", "az", "lo", "adr", "mo", "free")
+ORDER = ("fetch", "moments", "first", "outer", "inner", "last", "cross", "step", "pass0", "hop1", "hop2", "hop3", "over")
+KEYS = ("s", "d", "rb", "wb", "gb", "wl", "ml", "vl", "ld", "dr", "ds", "ss", "rr", "ar", "ad", "ay", "az", "lo", "adr", "mo", "mw", "free")
 
 
 def new_moments(m, v, g):
@@ -31,14 +31,14 @@
 
 
 def piece(which, r):
-    layer, q = r // 4, lax.rem(r, 4)
-    if which == 2:
-        return layer, pl.ds(pl.multiple_of(q // 2 * 112, 112), 112), pl.ds(pl.multiple_of(lax.rem(q, 2) * 512, 512), 512)
-    return layer, pl.ds(pl.multiple_of(q * 16, 16), 16), pl.ds(0, 3584)
+    rows, cols = shape_of(which)
+    across = (1024 if which == 2 else 3584) // cols
+    layer, q = r // (ROUNDS // 2), lax.rem(r, ROUNDS // 2)
+    return layer, pl.ds(pl.multiple_of(q // across * rows, rows), rows), pl.ds(pl.multiple_of(lax.rem(q, across) * cols, cols), cols)
 
 
 def shape_of(which):
-    return (112, 512) if which == 2 else (16, 3584)
+    return (112, 4096 // ROUNDS) if which == 2 else (16, 28672 // ROUNDS)
 
 
 def scratch(which):
@@ -49,7 +49,7 @@
         pltpu.VMEM((SLOTS, 8, rows, cols), bf),
         pltpu.VMEM((ROUNDS, 9 if which == 0 else 11, rows, cols), bf),
         pltpu.VMEM((ROUNDS, rows, cols), bf),
-        pltpu.VMEM((ROUNDS, rows, cols), bf),
+        pltpu.VMEM((rows, cols), bf),
         pltpu.VMEM((LOADS, rows, cols), bf),
         pltpu.VMEM((LOADS, rows, cols), f32),
         pltpu.VMEM((LOADS, rows, cols), f32),
@@ -65,6 +65,7 @@
         dma,
         dma,
         dma((LOADS, 3)),
+        dma((LOADS, 2)),
         pltpu.SemaphoreType.REGULAR,
     )
 
@@ -89,13 +90,13 @@
     f = (z + 1 - 2 * odd, 2 - z // 2, 3 * low)
     f_to = (onward, me + 2 - 4 * low, me + 2 - 4 * low)
 
-    inputs, outputs, rest = refs[:12], refs[12:18], refs[18:]
+    inputs, outputs, rest = refs[:12], refs[12:21], refs[21:]
     weights = []
     for i in range(3):
         x = Weight()
         x.which, x.types = i, TYPES[i]
         x.g, x.w, x.m, x.v = inputs[i], inputs[3 + i], inputs[6 + i], inputs[9 + i]
-        x.out, x.gout = outputs[i], outputs[3 + i]
+        x.out, x.mout, x.vout = outputs[i], outputs[3 + i], outputs[6 + i]
         for key, ref in zip(KEYS, rest[i * len(KEYS) : (i + 1) * len(KEYS)], strict=True):
             setattr(x, key, ref)
         weights.append(x)
@@ -118,15 +119,10 @@
         return ref.at[layer, rows, cols]
 
     def add(x, dst, *terms):
-        def slab(k, carry):
-            rows = pl.ds(pl.multiple_of(k * 16, 16), 16)
-            total = terms[0][rows, :].astype(jnp.float32)
-            for term in terms[1:]:
-                total += term[rows, :].astype(jnp.float32)
-            dst[rows, :] = total.astype(jnp.bfloat16)
-            return carry
-
-        lax.fori_loop(0, shape_of(x.which)[0] // 16, slab, 0)
+        total = terms[0][...].astype(jnp.float32)
+        for term in terms[1:]:
+            total += term[...].astype(jnp.float32)
+        dst[...] = total.astype(jnp.bfloat16)
 
     def ends(x, r, base):
         def when(then):
@@ -155,9 +151,21 @@
         pltpu.make_async_copy(blocks(x, x.g, r, slice(None), c), x.s.at[slot], x.ld.at[slot]).start()
         send(blocks(x, x.g, r, slice(None), 1 - c), x.d.at[slot], x.ds, x.dr.at[slot], partner).start()
 
+    def written(x, r, slot):
+        return (
+            pltpu.make_async_copy(x.ml.at[slot], mine(x, x.mout, r), x.mw.at[slot, 0]),
+            pltpu.make_async_copy(x.vl.at[slot], mine(x, x.vout, r), x.mw.at[slot, 1]),
+        )
+
     def moments(x, kind, r):
         slot = lax.rem(r, LOADS)
         layer, rows, cols = piece(x.which, r)
+
+        @pl.when(r >= LOADS)
+        def _():
+            for one in written(x, r, slot):
+                one.wait()
+
         pltpu.make_async_copy(x.w.at[layer, own, c, rows, cols], x.wl.at[slot], x.mo.at[slot, 0]).start()
         pltpu.make_async_copy(mine(x, x.m, r), x.ml.at[slot], x.mo.at[slot, 1]).start()
         pltpu.make_async_copy(mine(x, x.v, r), x.vl.at[slot], x.mo.at[slot, 2]).start()
@@ -167,59 +175,44 @@
         to = base + e_slot[k]
         send(x.s.at[slot, j], x.rb.at[r, to], x.ss.at[slot], x.rr.at[r, to], e_to[k]).start()
 
+    def ready(x, r, slot):
+        pltpu.make_async_copy(blocks(x, x.g, r, slice(None), c), x.s.at[slot], x.ld.at[slot]).wait()
+        arrive(x.d.at[slot], x.dr.at[slot])
+
     def first(x, kind, r):
         slot = lax.rem(r, SLOTS)
-        pltpu.make_async_copy(blocks(x, x.g, r, slice(None), c), x.s.at[slot], x.ld.at[slot]).wait()
-        arrive(x.d.at[slot], x.dr.at[slot])
-        if kind == "y":
-            for col in (*e, z):
-                j = (1 - y) * 4 + col
-                add(x, x.s.at[slot, j], x.s.at[slot, j], x.d.at[slot, j])
-                send(x.s.at[slot, j], x.rb.at[r, col], x.ss.at[slot], x.rr.at[r, col], across).start()
-        else:
-
-            @pl.when(corner)
-            def _():
-                for row in (1 - y, y):
-                    for k in range(3):
-                        j = row * 4 + e[k]
-                        add(x, x.s.at[slot, j], x.s.at[slot, j], x.d.at[slot, j])
-                        along(x, r, slot, row, k, row * 5)
-
-    def hops(x, kind, r, ks):
+        ready(x, r, slot)
+        for col in (*e, z):
+            j = (1 - y) * 4 + col
+            add(x, x.s.at[slot, j], x.s.at[slot, j], x.d.at[slot, j])
+            send(x.s.at[slot, j], x.rb.at[r, col], x.ss.at[slot], x.rr.at[r, col], across).start()
+
+    def onto(x, kind, r, ks, inner):
         slot = lax.rem(r, SLOTS)
-        if kind == "y":
+        for row in (y,) if kind == "y" else (1 - y, y):
+            base = 4 if kind == "y" else row * 5
             for k in ks:
-                j = y * 4 + e[k]
-                arrive(x.rb.at[r, e[k]], x.rr.at[r, e[k]])
-
-                @pl.when(mid)
-                def _():
-                    arrive(x.rb.at[r, 4 + e[k]], x.rr.at[r, 4 + e[k]])
-                    add(x, x.s.at[slot, j], x.s.at[slot, j], x.d.at[slot, j], x.rb.at[r, e[k]], x.rb.at[r, 4 + e[k]])
-
-                @pl.when(corner)
-                def _():
-                    add(x, x.s.at[slot, j], x.s.at[slot, j], x.d.at[slot, j], x.rb.at[r, e[k]])
-
-                along(x, r, slot, y, k, 4)
-        else:
-
-            @pl.when(mid)
-            def _():
-                for row in (1 - y, y):
-                    for k in ks:
-                        j = row * 4 + e[k]
-                        at = row * 5 + e[k]
-                        arrive(x.rb.at[r, at], x.rr.at[r, at])
-                        add(x, x.s.at[slot, j], x.s.at[slot, j], x.d.at[slot, j], x.rb.at[r, at])
-                        along(x, r, slot, row, k, row * 5)
-
-    def near(x, kind, r):
-        hops(x, kind, r, (0, 1))
-
-    def far(x, kind, r):
-        hops(x, kind, r, (2,))
+                j = row * 4 + e[k]
+                terms = [x.s.at[slot, j], x.d.at[slot, j]]
+                if kind == "y":
+                    arrive(x.rb.at[r, e[k]], x.rr.at[r, e[k]])
+                    terms.append(x.rb.at[r, e[k]])
+                if inner:
+                    arrive(x.rb.at[r, base + e[k]], x.rr.at[r, base + e[k]])
+                    terms.append(x.rb.at[r, base + e[k]])
+                add(x, x.s.at[slot, j], *terms)
+                along(x, r, slot, row, k, base)
+
+    def outer(x, kind, r):
+        if kind == "z":
+            ready(x, r, lax.rem(r, SLOTS))
+        pl.when(corner)(lambda: onto(x, kind, r, (0, 1, 2), False))
+
+    def inner(x, kind, r):
+        pl.when(mid)(lambda: onto(x, kind, r, (0, 1), True))
+
+    def last(x, kind, r):
+        pl.when(mid)(lambda: onto(x, kind, r, (2,), True))
 
     def cross(x, kind, r):
         slot = lax.rem(r, SLOTS)
@@ -249,22 +242,20 @@
         over = z if kind == "y" else 10
         arrive(x.rb.at[r, over], x.rr.at[r, over])
         base = 4 if kind == "y" else y * 5
-        ends(x, r, base)(lambda *got: add(x, x.gb.at[r], x.s.at[slot, own], x.d.at[slot, own], x.rb.at[r, over], *got))
+        ends(x, r, base)(lambda *got: add(x, x.gb, x.s.at[slot, own], x.d.at[slot, own], x.rb.at[r, over], *got))
         layer, rows, cols = piece(x.which, r)
         pltpu.make_async_copy(x.w.at[layer, own, c, rows, cols], x.wl.at[at], x.mo.at[at, 0]).wait()
         pltpu.make_async_copy(mine(x, x.m, r), x.ml.at[at], x.mo.at[at, 1]).wait()
         pltpu.make_async_copy(mine(x, x.v, r), x.vl.at[at], x.mo.at[at, 2]).wait()
 
-        def slab(k, carry):
-            rows = pl.ds(pl.multiple_of(k * 16, 16), 16)
-            m, v = new_moments(x.ml[at, rows, :], x.vl[at, rows, :], x.gb[r, rows, :].astype(jnp.float32))
-            x.wb[r, rows, :] = new_weight(x.wl[at, rows, :].astype(jnp.float32), m, v)
-            return carry
-
-        lax.fori_loop(0, shape_of(x.which)[0] // 16, slab, 0)
+        m, v = new_moments(x.ml[at], x.vl[at], x.gb[...].astype(jnp.float32))
+        x.ml[at] = m
+        x.vl[at] = v
+        x.wb[r] = new_weight(x.wl[at].astype(jnp.float32), m, v)
         share(x, kind, r, x.wb.at[r], own, True, True)
         pltpu.make_async_copy(x.wb.at[r], blocks(x, x.out, r, own, c), x.lo).start()
-        pltpu.make_async_copy(x.gb.at[r], mine(x, x.gout, r), x.lo).start()
+        for one in written(x, r, at):
+            one.start()
 
         @pl.when(r < ROUNDS - SLOTS)
         def _():
@@ -278,31 +269,33 @@
         j = (1 - y) * 4 + z
         share(x, kind, r, came(x, r, j), j, False, True)
 
-    def passes(x, kind, r, ks):
+    def passes(x, kind, r, ks, inner):
         t = 0 if kind == "y" else 1
         for row in (y,) if kind == "y" else (y, 1 - y):
             for k in ks:
                 j = row * 4 + f[k]
                 src = came(x, r, j)
-
-                @pl.when(mid)
-                def _():
+                if inner:
                     send(src, src, x.az.at[t], x.ar.at[r, j], f_to[k]).start()
-
                 share(x, kind, r, src, j, kind == "y", False)
 
-    def pass1(x, kind, r):
-        passes(x, kind, r, (0, 1))
-
-    def pass2(x, kind, r):
-        passes(x, kind, r, (2,))
-
-    def pass3(x, kind, r):
+    def hop1(x, kind, r):
+        pl.when(mid)(lambda: passes(x, kind, r, (0, 1), True))
+        pl.when(corner)(lambda: passes(x, kind, r, (0,), False))
+
+    def hop2(x, kind, r):
+        pl.when(mid)(lambda: passes(x, kind, r, (2,), True))
+        pl.when(corner)(lambda: passes(x, kind, r, (1,), False))
+
+    def hop3(x, kind, r):
+        pl.when(corner)(lambda: passes(x, kind, r, (2,), False))
+
+    def over(x, kind, r):
         for col in (z, *f):
             j = (1 - y) * 4 + col
             share(x, kind, r, came(x, r, j), j, False, False)
 
-    stages = {one.__name__: one for one in (fetch, moments, first, near, far, cross, step, pass0, pass1, pass2, pass3)}
+    stages = {one.__name__: one for one in (fetch, moments, first, outer, inner, last, cross, step, pass0, hop1, hop2, hop3, over)}
 
     barrier = pltpu.get_barrier_semaphore()
     pl.semaphore_signal(barrier, inc=1, device_id=(rep, partner), device_id_type=MESH)
@@ -328,7 +321,7 @@
         for sub in range(3):
             for name in ORDER:
                 for kind in ("y", "z"):
-                    lag = dict(LAGS[kind]).get(name)
+                    lag = LAGS[kind].get(name)
                     if lag is None:
                         continue
                     x = weights[(sub - lag) % 3]
@@ -342,7 +335,7 @@
                     pl.when(ok)(functools.partial(stages[name], x, kind, r))
         return carry
 
-    longest = max(lag for kind in LAGS.values() for _, lag in kind)
+    longest = max(max(kind.values()) for kind in LAGS.values())
     lax.fori_loop(0, ROUNDS + (longest + 2) // 3, turn, 0)
 
     for x in weights:
@@ -367,7 +360,10 @@
         left(x.rb.at[:, pl.ds(0, 8)], x.ds)
         left(x.rb.at[:, pl.ds(0, 8)], x.ad)
         arrive(x.rb.at[:, pl.ds(0, 8)], x.adr)
-        arrive(x.rb.at[:, pl.ds(0, 2)], x.lo)
+        arrive(x.rb.at[:, pl.ds(0, 1)], x.lo)
+        for r in range(ROUNDS - LOADS, ROUNDS):
+            for one in written(x, jnp.int32(r), r % LOADS):
+                one.wait()
 
 
 def solution(mesh):
@@ -381,16 +377,15 @@
         wide = [cut(one) for one in weights]
         outs = pl.pallas_call(
             kernel,
-            out_shape=[jax.ShapeDtypeStruct(one.shape, jnp.bfloat16) for one in (*wide, *m)],
+            out_shape=[jax.ShapeDtypeStruct(one.shape, one.dtype) for one in (*wide, *m, *v)],
             in_specs=[ANY] * 12,
-            out_specs=[ANY] * 6,
+            out_specs=[ANY] * 9,
             scratch_shapes=[one for i in range(3) for one in scratch(i)],
             compiler_params=pltpu.CompilerParams(collective_id=0, has_side_effects=True, vmem_limit_bytes=67043328),
             name="sum_step_gather",
         )(*(cut(t[0]) for t in terms), *wide, *m, *v)
         whole = [one.reshape(w.shape) for one, w in zip(outs[:3], weights, strict=True)]
-        new = [new_moments(*mvg) for mvg in zip(m, v, (g.astype(jnp.float32) for g in outs[3:]), strict=True)]
-        return (*whole, *(one[0] for one in new), *(one[1] for one in new))
+        return (*whole, *outs[3:])
 
     all_of, cut = P(None, None, None), P(None, "dp", None)
     return jax.shard_map(

time: 514 us -> 433 us (0.84)
  Pallas kernels: 476 us -> 389 us
  local copies, waits for them, and re-layouts: 23.9 us -> 42.1 us
  other arithmetic: 13.8 us -> 0.01 us
    pallas_call x1, Pallas kernels: 476 us -> 389 us  [step(): pl.pallas_call(kernel, out_shape=[jax.ShapeDtypeStruct(one.shape, one.dty...]
    unnamed x21 -> x31, local copies, waits for them, and re-layouts: 23.9 us -> 42.1 us
    add x2 -> x0, other arithmetic: 13.8 us -> none  [new_moments(): return (0.9 * m + 0.1 * g, 0.95 * v + 0.05 * g * g)]
where the time goes in v2:
time: 433 us; the launch traced here: 432 us
  Pallas kernels  389 us (90%)
  local copies, waits for them, and re-layouts  42.1 us (10%)
    pallas_call x1, Pallas kernels, step(): pl.pallas_call(kernel, out_shape=[jax.ShapeDtypeStruct(one.shape, one.dty...  389 us
    unnamed x31, local copies, waits for them, and re-layouts  42.1 us

profile of v2, /device:TPU:0, one launch (start us, length us, event | category | flops | bytes accessed | tf_op | source)
XLA Modules:
  0.0 432.2 jit_solution(1947682810723886049)
XLA Ops:
  0.6 389.4 %sum_step_gather.1 = (bf16[2,8,2,64,3584]{4,3,2,1,0:T(8,128)(2,1)}, bf16[2,8,2,64,3584]{4,3,2,1,0:T(8,128)(2,1)}, bf16[2,8,2,224,1024]{4,3,2,1,0:T(8,128)(2,1)},...) custom-call(bf16[2,8,2,64,3584]{4,3,2,1,0:T(8,128)(2,1)} %bitcast.14, ...), custom_call_target="tpu_custom_call" | custom-call | tf_op jit(solution)/shard_map/sum_step_gather/pallas_call | solution.py:378
  390.0 0.0 copy-start
  390.0 0.0 slice-start
  390.1 0.0 slice-start.1
  390.1 15.7 %copy.30 = bf16[2,1024,3584]{2,1,0:T(8,128)(2,1)} copy(bf16[2,1024,3584]{2,1,0:T(8,128)(2,1)} %bitcast.13) | data formatting | bytes 29360128
  405.8 0.0 copy-done
  405.8 0.0 slice-start.2
  405.8 0.0 slice-start.3
  405.8 7.4 %copy.31 = bf16[2,1024,3584]{2,1,0:T(8,128)(2,1)} copy(bf16[2,1024,3584]{2,1,0:T(8,128)(2,1)S(1)} %bitcast.12) | data formatting | bytes 29360128
  413.2 0.0 slice-done
  413.2 0.0 slice-done.1
  413.2 0.0 slice-done.2
  413.3 1.4 slice-done.3
  414.7 0.0 copy-start.6
  414.7 5.5 %copy.32 = bf16[2,3584,1024]{2,1,0:T(8,128)(2,1)} copy(bf16[2,3584,1024]{2,1,0:T(8,128)(2,1)S(1)} %bitcast.11) | data formatting | bytes 29360128
  420.2 0.0 copy-done.6
  420.2 0.0 copy-start.5
  420.2 1.2 copy.33
  421.4 0.9 copy-done.5
  422.3 0.0 copy-start.4
  422.3 1.2 copy.34
  423.6 0.9 copy-done.4
  424.5 0.0 copy-start.3
  424.5 1.2 copy.35
  425.7 0.9 copy-done.3
  426.6 0.0 copy-start.2
  426.6 1.2 copy.36
  427.9 0.9 copy-done.2
  428.8 0.0 copy-start.1
  428.8 1.2 copy.37
  430.0 0.9 copy-done.1
  431.0 1.2 copy.38
  (1 shorter events, 0.0 us)
Async XLA Ops:
  390.0 15.8 %copy-start = (bf16[2,8,2,64,3584]{4,3,2,1,0:T(8,128)(2,1)S(1)}, bf16[2,8,2,64,3584]{4,3,2,1,0:T(8,128)(2,1)}, u32[]{:S(2)}) copy-start(bf16[2,8,2,64,3584]{4,3,2,1,0:T(8,128)(2,1)} %get-tuple-element.19) | copy-start | bytes 44040196
  390.0 23.2 %slice-start = ((s8[14680064]{0:T(1024)(128)(4,1)}), s8[4194304]{0:T(1024)(128)(4,1)S(1)}, s32[]{:S(2)}) async-start(s8[14680064]{0:T(1024)(128)(4,1)} %bitcast.9), calls=%async_computation | async-start | bytes 8388608
  390.1 23.2 %slice-start.1 = ((s8[14680064]{0:T(1024)(128)(4,1)}), s8[4194304]{0:T(1024)(128)(4,1)S(1)}, s32[]{:S(2)}) async-start(s8[14680064]{0:T(1024)(128)(4,1)} %bitcast.9), calls=%async_computation.1 | async-start | bytes 8388608
  405.8 7.5 %slice-start.2 = ((s8[14680064]{0:T(1024)(128)(4,1)}), s8[4194304]{0:T(1024)(128)(4,1)S(1)}, s32[]{:S(2)}) async-start(s8[14680064]{0:T(1024)(128)(4,1)} %bitcast.9), calls=%async_computation.2 | async-start | bytes 8388608
  405.8 8.9 %slice-start.3 = ((s8[14680064]{0:T(1024)(128)(4,1)}), s8[2097152]{0:T(1024)(128)(4,1)S(1)}, s32[]{:S(2)}) async-start(s8[14680064]{0:T(1024)(128)(4,1)} %bitcast.9), calls=%async_computation.3 | async-start | bytes 4194304
  414.7 5.5 %copy-start.6 = (f32[2,64,3584]{2,1,0:T(8,128)S(1)}, f32[2,64,3584]{2,1,0:T(8,128)}, u32[]{:S(2)}) copy-start(f32[2,64,3584]{2,1,0:T(8,128)} %get-tuple-element.39) | copy-start | bytes 5505028
  420.2 2.2 copy-start.5
  422.3 2.2 copy-start.4
  424.5 2.2 copy-start.3
  426.6 2.2 copy-start.2
  428.8 2.2 copy-start.1

commit v3 on v2

--- a/solution.py
+++ b/solution.py
@@ -9,17 +9,19 @@
 
 MESH = pl.DeviceIdType.MESH
 ANY = pl.BlockSpec(memory_space=pl.ANY)
-ROUNDS = 16
-SLOTS = 4
+ROUNDS = 32
+SLOTS = 5
+INBOX = 5
+HELD = (False, False, False)
 LOADS = 2
 NAMES = ("gate", "up", "down")
 TYPES = (("y",) * ROUNDS, ("z",) * ROUNDS, ("y", "y", "y", "z") * (ROUNDS // 4))
 LAGS = {
-    "y": {"fetch": 0, "first": 3, "outer": 4, "inner": 5, "last": 6, "moments": 5, "step": 7, "hop1": 8, "hop2": 9, "hop3": 10, "over": 11},
-    "z": {"fetch": 0, "outer": 3, "inner": 4, "last": 5, "cross": 6, "moments": 5, "step": 7, "pass0": 8, "hop1": 9, "hop2": 10, "hop3": 11},
+    "y": {"fetch": 0, "first": 2, "outer": 4, "inner": 6, "last": 8, "moments": 7, "step": 10, "hop1": 12, "hop2": 14, "hop3": 16, "over": 18},
+    "z": {"fetch": 0, "outer": 2, "inner": 4, "last": 6, "cross": 8, "moments": 7, "step": 10, "pass0": 12, "hop1": 14, "hop2": 16, "hop3": 18},
 }
 ORDER = ("fetch", "moments", "first", "outer", "inner", "last", "cross", "step", "pass0", "hop1", "hop2", "hop3", "over")
-KEYS = ("s", "d", "rb", "wb", "gb", "wl", "ml", "vl", "ld", "dr", "ds", "ss", "rr", "ar", "ad", "ay", "az", "lo", "adr", "mo", "mw", "free")
+KEYS = ("s", "d", "rb", "wb", "gb", "wl", "ml", "vl", "ld", "dr", "ds", "ss", "rr", "ar", "ad", "ay", "az", "adr", "mo", "mw", "lo", "free", "y_free", "on_free", "back_free")
 
 
 def new_moments(m, v, g):
@@ -39,6 +41,10 @@
 
 def shape_of(which):
     return (112, 4096 // ROUNDS) if which == 2 else (16, 28672 // ROUNDS)
+
+
+def block_of(which):
+    return (224, 1024) if which == 2 else (64, 3584)
 
 
 def scratch(which):
@@ -47,8 +53,8 @@
     return (
         pltpu.VMEM((SLOTS, 8, rows, cols), bf),
         pltpu.VMEM((SLOTS, 8, rows, cols), bf),
-        pltpu.VMEM((ROUNDS, 9 if which == 0 else 11, rows, cols), bf),
-        pltpu.VMEM((ROUNDS, rows, cols), bf),
+        pltpu.VMEM((INBOX, 9 if which == 0 else 11, rows, cols), bf),
+        pltpu.VMEM((1 if HELD[which] else ROUNDS, rows, cols), bf),
         pltpu.VMEM((rows, cols), bf),
         pltpu.VMEM((LOADS, rows, cols), bf),
         pltpu.VMEM((LOADS, rows, cols), f32),
@@ -57,16 +63,16 @@
         dma((SLOTS,)),
         dma,
         dma((SLOTS,)),
-        dma((ROUNDS, 11)),
+        dma((INBOX, 11)),
         dma((ROUNDS, 8)),
         dma,
         dma((2,)),
         dma((2,)),
         dma,
-        dma,
         dma((LOADS, 3)),
         dma((LOADS, 2)),
-        pltpu.SemaphoreType.REGULAR,
+        dma,
+        *([pltpu.SemaphoreType.REGULAR] * 4),
     )
 
 
@@ -128,15 +134,15 @@
         def when(then):
             @pl.when(mid)
             def _():
-                arrive(x.rb.at[r, base + z], x.rr.at[r, base + z])
-                arrive(x.rb.at[r, base + 4], x.rr.at[r, base + 4])
-                then(x.rb.at[r, base + z], x.rb.at[r, base + 4])
+                arrive(x.rb.at[lax.rem(r, INBOX), base + z], x.rr.at[lax.rem(r, INBOX), base + z])
+                arrive(x.rb.at[lax.rem(r, INBOX), base + 4], x.rr.at[lax.rem(r, INBOX), base + 4])
+                then(x.rb.at[lax.rem(r, INBOX), base + z], x.rb.at[lax.rem(r, INBOX), base + 4])
 
             @pl.when(corner)
             def _():
                 at = base + 4 - z // 3
-                arrive(x.rb.at[r, at], x.rr.at[r, at])
-                then(x.rb.at[r, at])
+                arrive(x.rb.at[lax.rem(r, INBOX), at], x.rr.at[lax.rem(r, INBOX), at])
+                then(x.rb.at[lax.rem(r, INBOX), at])
 
         return when
 
@@ -173,19 +179,26 @@
     def along(x, r, slot, row, k, base, *terms):
         j = row * 4 + e[k]
         to = base + e_slot[k]
-        send(x.s.at[slot, j], x.rb.at[r, to], x.ss.at[slot], x.rr.at[r, to], e_to[k]).start()
+        send(x.s.at[slot, j], x.rb.at[lax.rem(r, INBOX), to], x.ss.at[slot], x.rr.at[lax.rem(r, INBOX), to], e_to[k]).start()
 
     def ready(x, r, slot):
         pltpu.make_async_copy(blocks(x, x.g, r, slice(None), c), x.s.at[slot], x.ld.at[slot]).wait()
         arrive(x.d.at[slot], x.dr.at[slot])
 
+    def granted(r, free):
+        pl.when(r >= INBOX)(lambda: pl.semaphore_wait(free, 1))
+
+    def grant(free, to):
+        pl.semaphore_signal(free, inc=1, device_id=(rep, to), device_id_type=MESH)
+
     def first(x, kind, r):
         slot = lax.rem(r, SLOTS)
         ready(x, r, slot)
+        granted(r, x.y_free)
         for col in (*e, z):
             j = (1 - y) * 4 + col
             add(x, x.s.at[slot, j], x.s.at[slot, j], x.d.at[slot, j])
-            send(x.s.at[slot, j], x.rb.at[r, col], x.ss.at[slot], x.rr.at[r, col], across).start()
+            send(x.s.at[slot, j], x.rb.at[lax.rem(r, INBOX), col], x.ss.at[slot], x.rr.at[lax.rem(r, INBOX), col], across).start()
 
     def onto(x, kind, r, ks, inner):
         slot = lax.rem(r, SLOTS)
@@ -195,30 +208,41 @@
                 j = row * 4 + e[k]
                 terms = [x.s.at[slot, j], x.d.at[slot, j]]
                 if kind == "y":
-                    arrive(x.rb.at[r, e[k]], x.rr.at[r, e[k]])
-                    terms.append(x.rb.at[r, e[k]])
+                    arrive(x.rb.at[lax.rem(r, INBOX), e[k]], x.rr.at[lax.rem(r, INBOX), e[k]])
+                    terms.append(x.rb.at[lax.rem(r, INBOX), e[k]])
                 if inner:
-                    arrive(x.rb.at[r, base + e[k]], x.rr.at[r, base + e[k]])
-                    terms.append(x.rb.at[r, base + e[k]])
+                    arrive(x.rb.at[lax.rem(r, INBOX), base + e[k]], x.rr.at[lax.rem(r, INBOX), base + e[k]])
+                    terms.append(x.rb.at[lax.rem(r, INBOX), base + e[k]])
                 add(x, x.s.at[slot, j], *terms)
                 along(x, r, slot, row, k, base)
 
     def outer(x, kind, r):
         if kind == "z":
             ready(x, r, lax.rem(r, SLOTS))
-        pl.when(corner)(lambda: onto(x, kind, r, (0, 1, 2), False))
+
+        @pl.when(corner)
+        def _():
+            granted(r, x.on_free)
+            onto(x, kind, r, (0, 1, 2), False)
 
     def inner(x, kind, r):
-        pl.when(mid)(lambda: onto(x, kind, r, (0, 1), True))
+        @pl.when(mid)
+        def _():
+            granted(r, x.on_free)
+            onto(x, kind, r, (0, 1), True)
 
     def last(x, kind, r):
-        pl.when(mid)(lambda: onto(x, kind, r, (2,), True))
+        @pl.when(mid)
+        def _():
+            granted(r, x.back_free)
+            onto(x, kind, r, (2,), True)
 
     def cross(x, kind, r):
         slot = lax.rem(r, SLOTS)
         j = (1 - y) * 4 + z
         ends(x, r, (1 - y) * 5)(lambda *got: add(x, x.s.at[slot, j], x.s.at[slot, j], x.d.at[slot, j], *got))
-        send(x.s.at[slot, j], x.rb.at[r, 10], x.ss.at[slot], x.rr.at[r, 10], across).start()
+        granted(r, x.y_free)
+        send(x.s.at[slot, j], x.rb.at[lax.rem(r, INBOX), 10], x.ss.at[slot], x.rr.at[lax.rem(r, INBOX), 10], across).start()
 
     def share(x, kind, r, src, j, to_y, to_z):
         dst = blocks(x, x.out, r, j, c)
@@ -240,9 +264,9 @@
     def step(x, kind, r):
         slot, at = lax.rem(r, SLOTS), lax.rem(r, LOADS)
         over = z if kind == "y" else 10
-        arrive(x.rb.at[r, over], x.rr.at[r, over])
+        arrive(x.rb.at[lax.rem(r, INBOX), over], x.rr.at[lax.rem(r, INBOX), over])
         base = 4 if kind == "y" else y * 5
-        ends(x, r, base)(lambda *got: add(x, x.gb, x.s.at[slot, own], x.d.at[slot, own], x.rb.at[r, over], *got))
+        ends(x, r, base)(lambda *got: add(x, x.gb, x.s.at[slot, own], x.d.at[slot, own], x.rb.at[lax.rem(r, INBOX), over], *got))
         layer, rows, cols = piece(x.which, r)
         pltpu.make_async_copy(x.w.at[layer, own, c, rows, cols], x.wl.at[at], x.mo.at[at, 0]).wait()
         pltpu.make_async_copy(mine(x, x.m, r), x.ml.at[at], x.mo.at[at, 1]).wait()
@@ -251,15 +275,32 @@
         m, v = new_moments(x.ml[at], x.vl[at], x.gb[...].astype(jnp.float32))
         x.ml[at] = m
         x.vl[at] = v
-        x.wb[r] = new_weight(x.wl[at].astype(jnp.float32), m, v)
-        share(x, kind, r, x.wb.at[r], own, True, True)
-        pltpu.make_async_copy(x.wb.at[r], blocks(x, x.out, r, own, c), x.lo).start()
+        layer, rows, cols = piece(x.which, r)
+        new, place = new_weight(x.wl[at].astype(jnp.float32), m, v), blocks(x, x.out, r, own, c)
+        if HELD[x.which]:
+            x.out[layer, own, c, rows, cols] = new
+            share(x, kind, r, place, own, True, True)
+        else:
+            x.wb[r] = new
+            share(x, kind, r, x.wb.at[r], own, True, True)
+            pltpu.make_async_copy(x.wb.at[r], place, x.lo).start()
         for one in written(x, r, at):
             one.start()
 
-        @pl.when(r < ROUNDS - SLOTS)
-        def _():
-            pl.semaphore_signal(x.free, inc=1, device_id=(rep, partner), device_id_type=MESH)
+        pl.when(r < ROUNDS - SLOTS)(lambda: grant(x.free, partner))
+
+        @pl.when(r < ROUNDS - INBOX)
+        def _():
+            grant(x.y_free, across)
+
+            @pl.when(mid)
+            def _():
+                grant(x.on_free, onward)
+                grant(x.on_free, 2 * me - onward)
+
+            @pl.when(corner)
+            def _():
+                grant(x.back_free, onward)
 
     def came(x, r, j):
         arrive(blocks(x, x.out, r, j, c), x.ar.at[r, j])
@@ -342,25 +383,27 @@
         for slot in range(SLOTS):
             left(x.s.at[slot, pl.ds(0, 7)], x.ss.at[slot])
         for t, kind in enumerate(("y", "z")):
-            n = x.types.count(kind)
-            if n:
-                left(x.rb.at[pl.ds(0, n), pl.ds(0, 4 if kind == "y" else 1)], x.ay.at[t])
+            share_of = block_of(x.which)[1] * x.types.count(kind) // ROUNDS
+            if share_of:
+
+                def all_of(k):
+                    return x.out.at[:, pl.ds(0, k), 0, :, pl.ds(0, share_of)]
+
+                left(all_of(4 if kind == "y" else 1), x.ay.at[t])
 
                 @pl.when(mid)
                 def _():
-                    if kind == "y":
-                        left(x.rb.at[pl.ds(0, n), pl.ds(0, 5)], x.az.at[t])
-                    else:
-                        left(x.rb.at[pl.ds(0, n), pl.ds(0, 10)], x.az.at[t])
+                    left(all_of(5) if kind == "y" else x.out.at[:, pl.ds(0, 5), :, :, pl.ds(0, share_of)], x.az.at[t])
 
                 @pl.when(corner)
                 def _():
-                    left(x.rb.at[pl.ds(0, n), pl.ds(0, 1 if kind == "y" else 2)], x.az.at[t])
-
-        left(x.rb.at[:, pl.ds(0, 8)], x.ds)
-        left(x.rb.at[:, pl.ds(0, 8)], x.ad)
-        arrive(x.rb.at[:, pl.ds(0, 8)], x.adr)
-        arrive(x.rb.at[:, pl.ds(0, 1)], x.lo)
+                    left(all_of(1 if kind == "y" else 2), x.az.at[t])
+
+        left(x.out.at[:, :, 0], x.ds)
+        left(x.out.at[:, :, 0], x.ad)
+        arrive(x.out.at[:, :, 0], x.adr)
+        if not HELD[x.which]:
+            arrive(x.wb, x.lo)
         for r in range(ROUNDS - LOADS, ROUNDS):
             for one in written(x, jnp.int32(r), r % LOADS):
                 one.wait()
@@ -377,13 +420,13 @@
         wide = [cut(one) for one in weights]
         outs = pl.pallas_call(
             kernel,
-            out_shape=[jax.ShapeDtypeStruct(one.shape, one.dtype) for one in (*wide, *m, *v)],
+            out_shape=[*((pltpu.VMEM if held else jax.ShapeDtypeStruct)(one.shape, one.dtype) for held, one in zip(HELD, wide, strict=True)), *(pltpu.HBM(one.shape, one.dtype) for one in (*m, *v))],
             in_specs=[ANY] * 12,
-            out_specs=[ANY] * 9,
+            out_specs=[pl.BlockSpec(memory_space=pltpu.VMEM) if held else ANY for held in HELD] + [ANY] * 6,
             scratch_shapes=[one for i in range(3) for one in scratch(i)],
-            compiler_params=pltpu.CompilerParams(collective_id=0, has_side_effects=True, vmem_limit_bytes=67043328),
+            compiler_params=pltpu.CompilerParams(collective_id=0, has_side_effects=True, vmem_limit_bytes=16 * 2**20),
             name="sum_step_gather",
-        )(*(cut(t[0]) for t in terms), *wide, *m, *v)
+        )(*(pltpu.with_memory_space_constraint(one, pltpu.HBM) for one in (*(cut(t[0]) for t in terms), *wide, *m, *v)))
         whole = [one.reshape(w.shape) for one, w in zip(outs[:3], weights, strict=True)]
         return (*whole, *outs[3:])
 

time: 433 us -> 411 us (0.949)
  Pallas kernels: 389 us -> 377 us
  local copies, waits for them, and re-layouts: 42.1 us -> 33.5 us
    pallas_call x1, Pallas kernels: 389 us -> 377 us  [step(): pl.pallas_call(kernel, out_shape=[*((pltpu.VMEM if held else jax.ShapeDty...]
    unnamed x31 -> x23, local copies, waits for them, and re-layouts: 42.1 us -> 33.5 us
where the time goes in v3:
time: 411 us
  Pallas kernels  377 us (92%)
  local copies, waits for them, and re-layouts  33.5 us (8%)
    pallas_call x1, Pallas kernels, step(): pl.pallas_call(kernel, out_shape=[*((pltpu.VMEM if held else jax.ShapeDty...  377 us
    unnamed x23, local copies, waits for them, and re-layouts  33.5 us

profile of v3, /device:TPU:0, one launch (start us, length us, event | category | flops | bytes accessed | tf_op | source)
XLA Modules:
  0.0 410.8 jit_solution(16431382142829456577)
XLA Ops:
  0.6 376.7 %sum_step_gather.1 = (bf16[2,8,2,64,3584]{4,3,2,1,0:T(8,128)(2,1)S(1)}, bf16[2,8,2,64,3584]{4,3,2,1,0:T(8,128)(2,1)S(1)}, bf16[2,8,2,224,1024]{4,3,2,1,0:T(8,128...) custom-call(bf16[2,8,2,64,3584]{4,3,2,1,0:T(8,128)(2,1)} %bitcast.12, ...), custom_call_target="tpu_custom_call" | custom-call | tf_op jit(solution)/shard_map/sum_step_gather/pallas_call | solution.py:421
  377.3 5.5 %copy.30 = bf16[2,1024,3584]{2,1,0:T(8,128)(2,1)} copy(bf16[2,1024,3584]{2,1,0:T(8,128)(2,1)S(1)} %bitcast.10) | data formatting | bytes 29360128
  382.8 0.0 copy-start
  382.8 7.4 %copy.31 = bf16[2,1024,3584]{2,1,0:T(8,128)(2,1)} copy(bf16[2,1024,3584]{2,1,0:T(8,128)(2,1)S(1)} %bitcast.9) | data formatting | bytes 29360128
  390.2 3.0 copy-done
  393.3 0.0 copy-start.6
  393.3 5.5 %copy.32 = bf16[2,3584,1024]{2,1,0:T(8,128)(2,1)} copy(bf16[2,3584,1024]{2,1,0:T(8,128)(2,1)S(1)} %bitcast.11) | data formatting | bytes 29360128
  398.8 0.0 copy-done.6
  398.8 0.0 copy-start.5
  398.8 1.2 copy.33
  400.0 0.9 copy-done.5
  400.9 0.0 copy-start.4
  400.9 1.2 copy.34
  402.2 0.9 copy-done.4
  403.1 0.0 copy-start.3
  403.1 1.2 copy.35
  404.3 0.9 copy-done.3
  405.3 0.0 copy-start.2
  405.3 1.2 copy.36
  406.5 0.9 copy-done.2
  407.4 0.0 copy-start.1
  407.4 1.2 copy.37
  408.6 0.9 copy-done.1
  409.6 1.2 copy.38
Async XLA Ops:
  382.8 10.5 %copy-start = (bf16[2,8,2,224,1024]{4,3,2,1,0:T(8,128)(2,1)S(1)}, bf16[2,8,2,224,1024]{4,3,2,1,0:T(8,128)(2,1)}, u32[]{:S(2)}) copy-start(bf16[2,8,2,224,1024]{4,3,2,1,0:T(8,128)(2,1)} %get-tuple-element.20) | copy-start | bytes 44040196
  393.3 5.5 %copy-start.6 = (f32[2,64,3584]{2,1,0:T(8,128)S(1)}, f32[2,64,3584]{2,1,0:T(8,128)}, u32[]{:S(2)}) copy-start(f32[2,64,3584]{2,1,0:T(8,128)} %get-tuple-element.39) | copy-start | bytes 5505028
  398.8 2.2 copy-start.5
  400.9 2.2 copy-start.4
  403.1 2.2 copy-start.3
  405.3 2.2 copy-start.2
  407.4 2.2 copy-start.1

commit v4 on v3

--- a/solution.py
+++ b/solution.py
@@ -15,7 +15,18 @@
 HELD = (False, False, False)
 LOADS = 2
 NAMES = ("gate", "up", "down")
-TYPES = (("y",) * ROUNDS, ("z",) * ROUNDS, ("y", "y", "y", "z") * (ROUNDS // 4))
+ALONE = 6
+
+
+def kinds(which, r, gather):
+    among = r >= ALONE if not gather else r < ROUNDS - ALONE
+    if which == 0:
+        return ("y",), None
+    if which == 1:
+        return ("y", "z"), among | (lax.rem(r + ROUNDS, 2) == 1)
+    return ("y", "z"), among & (lax.rem(r + ROUNDS, 4) == 3)
+
+
 LAGS = {
     "y": {"fetch": 0, "first": 2, "outer": 4, "inner": 6, "last": 8, "moments": 7, "step": 10, "hop1": 12, "hop2": 14, "hop3": 16, "over": 18},
     "z": {"fetch": 0, "outer": 2, "inner": 4, "last": 6, "cross": 8, "moments": 7, "step": 10, "pass0": 12, "hop1": 14, "hop2": 16, "hop3": 18},
@@ -41,10 +52,6 @@
 
 def shape_of(which):
     return (112, 4096 // ROUNDS) if which == 2 else (16, 28672 // ROUNDS)
-
-
-def block_of(which):
-    return (224, 1024) if which == 2 else (64, 3584)
 
 
 def scratch(which):
@@ -66,8 +73,8 @@
         dma((INBOX, 11)),
         dma((ROUNDS, 8)),
         dma,
-        dma((2,)),
-        dma((2,)),
+        dma((ROUNDS,)),
+        dma((ROUNDS,)),
         dma,
         dma((LOADS, 3)),
         dma((LOADS, 2)),
@@ -78,6 +85,9 @@
 
 class Weight:
     pass
+
+
+GATHER = ("pass0", "hop1", "hop2", "hop3", "over")
 
 
 def kernel(*refs):
@@ -100,7 +110,7 @@
     weights = []
     for i in range(3):
         x = Weight()
-        x.which, x.types = i, TYPES[i]
+        x.which = i
         x.g, x.w, x.m, x.v = inputs[i], inputs[3 + i], inputs[6 + i], inputs[9 + i]
         x.out, x.mout, x.vout = outputs[i], outputs[3 + i], outputs[6 + i]
         for key, ref in zip(KEYS, rest[i * len(KEYS) : (i + 1) * len(KEYS)], strict=True):
@@ -219,6 +229,7 @@
     def outer(x, kind, r):
         if kind == "z":
             ready(x, r, lax.rem(r, SLOTS))
+            granted(r, x.y_free)
 
         @pl.when(corner)
         def _():
@@ -241,23 +252,21 @@
         slot = lax.rem(r, SLOTS)
         j = (1 - y) * 4 + z
         ends(x, r, (1 - y) * 5)(lambda *got: add(x, x.s.at[slot, j], x.s.at[slot, j], x.d.at[slot, j], *got))
-        granted(r, x.y_free)
         send(x.s.at[slot, j], x.rb.at[lax.rem(r, INBOX), 10], x.ss.at[slot], x.rr.at[lax.rem(r, INBOX), 10], across).start()
 
     def share(x, kind, r, src, j, to_y, to_z):
         dst = blocks(x, x.out, r, j, c)
-        t = 0 if kind == "y" else 1
         if to_y:
-            send(src, dst, x.ay.at[t], x.ar.at[r, j], across).start()
+            send(src, dst, x.ay.at[r], x.ar.at[r, j], across).start()
         if to_z:
 
             @pl.when(z < 3)
             def _():
-                send(src, dst, x.az.at[t], x.ar.at[r, j], me + 2).start()
+                send(src, dst, x.az.at[r], x.ar.at[r, j], me + 2).start()
 
             @pl.when(z > 0)
             def _():
-                send(src, dst, x.az.at[t], x.ar.at[r, j], me - 2).start()
+                send(src, dst, x.az.at[r], x.ar.at[r, j], me - 2).start()
 
         send(src, dst, x.ad, x.adr, partner).start()
 
@@ -311,13 +320,12 @@
         share(x, kind, r, came(x, r, j), j, False, True)
 
     def passes(x, kind, r, ks, inner):
-        t = 0 if kind == "y" else 1
         for row in (y,) if kind == "y" else (y, 1 - y):
             for k in ks:
                 j = row * 4 + f[k]
                 src = came(x, r, j)
                 if inner:
-                    send(src, src, x.az.at[t], x.ar.at[r, j], f_to[k]).start()
+                    send(src, src, x.az.at[r], x.ar.at[r, j], f_to[k]).start()
                 share(x, kind, r, src, j, kind == "y", False)
 
     def hop1(x, kind, r):
@@ -366,13 +374,16 @@
                     if lag is None:
                         continue
                     x = weights[(sub - lag) % 3]
-                    if kind not in x.types:
-                        continue
                     r = i + (sub - lag) // 3
                     ok = (r >= 0) & (r < ROUNDS)
-                    if len(set(x.types)) > 1:
-                        last = lax.rem(r + 4, 4) == 3
-                        ok = ok & (last if kind == "z" else jnp.logical_not(last))
+                    some, is_z = kinds(x.which, r, name in GATHER)
+                    if name in ("fetch", "moments"):
+                        if kind == "z":
+                            continue
+                    elif kind not in some:
+                        continue
+                    elif is_z is not None:
+                        ok = ok & (is_z if kind == "z" else jnp.logical_not(is_z))
                     pl.when(ok)(functools.partial(stages[name], x, kind, r))
         return carry
 
@@ -382,23 +393,19 @@
     for x in weights:
         for slot in range(SLOTS):
             left(x.s.at[slot, pl.ds(0, 7)], x.ss.at[slot])
-        for t, kind in enumerate(("y", "z")):
-            share_of = block_of(x.which)[1] * x.types.count(kind) // ROUNDS
-            if share_of:
-
-                def all_of(k):
-                    return x.out.at[:, pl.ds(0, k), 0, :, pl.ds(0, share_of)]
-
-                left(all_of(4 if kind == "y" else 1), x.ay.at[t])
-
-                @pl.when(mid)
-                def _():
-                    left(all_of(5) if kind == "y" else x.out.at[:, pl.ds(0, 5), :, :, pl.ds(0, share_of)], x.az.at[t])
-
-                @pl.when(corner)
-                def _():
-                    left(all_of(1 if kind == "y" else 2), x.az.at[t])
-
+        def gathered(r, carry):
+            some, is_z = kinds(x.which, r, True)
+            for kind in some:
+
+                def sent():
+                    left(x.s.at[0, pl.ds(0, 4 if kind == "y" else 1)], x.ay.at[r])
+                    pl.when(mid)(lambda: left(x.s.at[pl.ds(0, 1 if kind == "y" else 2), pl.ds(0, 5)], x.az.at[r]))
+                    pl.when(corner)(lambda: left(x.s.at[0, pl.ds(0, 1 if kind == "y" else 2)], x.az.at[r]))
+
+                pl.when(True if is_z is None else is_z if kind == "z" else jnp.logical_not(is_z))(sent)
+            return carry
+
+        lax.fori_loop(0, ROUNDS, gathered, 0)
         left(x.out.at[:, :, 0], x.ds)
         left(x.out.at[:, :, 0], x.ad)
         arrive(x.out.at[:, :, 0], x.adr)

time: 411 us -> 404 us (0.983)
  Pallas kernels: 377 us -> 370 us
    pallas_call x1, Pallas kernels: 377 us -> 370 us  [step(): pl.pallas_call(kernel, out_shape=[*((pltpu.VMEM if held else jax.ShapeDty...]
where the time goes in v4:
time: 404 us
  Pallas kernels  370 us (92%)
  local copies, waits for them, and re-layouts  33.5 us (8%)
    pallas_call x1, Pallas kernels, step(): pl.pallas_call(kernel, out_shape=[*((pltpu.VMEM if held else jax.ShapeDty...  370 us
    unnamed x23, local copies, waits for them, and re-layouts  33.5 us

profile of v4, /device:TPU:0, one launch (start us, length us, event | category | flops | bytes accessed | tf_op | source)
XLA Modules:
  0.0 403.9 jit_solution(356563734756158079)
XLA Ops:
  0.6 369.8 %sum_step_gather.1 = (bf16[2,8,2,64,3584]{4,3,2,1,0:T(8,128)(2,1)S(1)}, bf16[2,8,2,64,3584]{4,3,2,1,0:T(8,128)(2,1)S(1)}, bf16[2,8,2,224,1024]{4,3,2,1,0:T(8,128...) custom-call(bf16[2,8,2,64,3584]{4,3,2,1,0:T(8,128)(2,1)} %bitcast.12, ...), custom_call_target="tpu_custom_call" | custom-call | tf_op jit(solution)/shard_map/sum_step_gather/pallas_call | solution.py:428
  370.5 5.5 %copy.30 = bf16[2,1024,3584]{2,1,0:T(8,128)(2,1)} copy(bf16[2,1024,3584]{2,1,0:T(8,128)(2,1)S(1)} %bitcast.10) | data formatting | bytes 29360128
  375.9 0.0 copy-start
  375.9 7.4 %copy.31 = bf16[2,1024,3584]{2,1,0:T(8,128)(2,1)} copy(bf16[2,1024,3584]{2,1,0:T(8,128)(2,1)S(1)} %bitcast.9) | data formatting | bytes 29360128
  383.4 3.0 copy-done
  386.4 0.0 copy-start.6
  386.4 5.5 %copy.32 = bf16[2,3584,1024]{2,1,0:T(8,128)(2,1)} copy(bf16[2,3584,1024]{2,1,0:T(8,128)(2,1)S(1)} %bitcast.11) | data formatting | bytes 29360128
  391.9 0.0 copy-done.6
  391.9 0.0 copy-start.5
  391.9 1.2 copy.33
  393.1 0.9 copy-done.5
  394.1 0.0 copy-start.4
  394.1 1.2 copy.34
  395.3 0.9 copy-done.4
  396.2 0.0 copy-start.3
  396.2 1.2 copy.35
  397.5 0.9 copy-done.3
  398.4 0.0 copy-start.2
  398.4 1.2 copy.36
  399.6 0.9 copy-done.2
  400.6 0.0 copy-start.1
  400.6 1.2 copy.37
  401.8 0.9 copy-done.1
  402.7 1.2 copy.38
Async XLA Ops:
  375.9 10.5 %copy-start = (bf16[2,8,2,224,1024]{4,3,2,1,0:T(8,128)(2,1)S(1)}, bf16[2,8,2,224,1024]{4,3,2,1,0:T(8,128)(2,1)}, u32[]{:S(2)}) copy-start(bf16[2,8,2,224,1024]{4,3,2,1,0:T(8,128)(2,1)} %get-tuple-element.20) | copy-start | bytes 44040196
  386.4 5.5 %copy-start.6 = (f32[2,64,3584]{2,1,0:T(8,128)S(1)}, f32[2,64,3584]{2,1,0:T(8,128)}, u32[]{:S(2)}) copy-start(f32[2,64,3584]{2,1,0:T(8,128)} %get-tuple-element.39) | copy-start | bytes 5505028
  391.9 2.2 copy-start.5
  394.1 2.2 copy-start.4
  396.2 2.2 copy-start.3
  398.4 2.2 copy-start.2
  400.6 2.2 copy-start.1

commit v5 on v4

--- a/solution.py
+++ b/solution.py
@@ -13,6 +13,7 @@
 SLOTS = 5
 INBOX = 5
 HELD = (False, False, False)
+RING = 4
 LOADS = 2
 NAMES = ("gate", "up", "down")
 ALONE = 6
@@ -416,6 +417,38 @@
                 one.wait()
 
 
+def finish(*refs):
+    ins, outs, stages, ring = refs[:9], refs[9:18], refs[18:24], refs[24]
+    sent, loaded, stored, taken, given = refs[25:]
+    puts = []
+    for i in range(2):
+        rows = outs[i].shape[1] // 4
+        for k in range(8):
+            part = (k // 4, pl.ds(k % 4 * rows, rows))
+            puts.append(pltpu.make_async_copy(ins[i].at[part], outs[i].at[part], sent.at[i, k]))
+    loads = [pltpu.make_async_copy(ins[3 + i], stages[i], loaded.at[i]) for i in range(6)]
+    stores = [pltpu.make_async_copy(stages[i], outs[3 + i], stored.at[i]) for i in range(6)]
+    takes, gives = [], []
+    rows = ring.shape[1]
+    for k in range(2 * (3584 // rows)):
+        part, slot = (k // (3584 // rows), pl.ds(k % (3584 // rows) * rows, rows)), k % RING
+        takes.append(pltpu.make_async_copy(ins[2].at[part], ring.at[slot], taken.at[slot]))
+        gives.append(pltpu.make_async_copy(ring.at[slot], outs[2].at[part], given.at[slot]))
+    for one in (*takes[:RING], *loads[:2], *puts, *loads[2:]):
+        one.start()
+    for k, (take, give) in enumerate(zip(takes, gives, strict=True)):
+        take.wait()
+        give.start()
+        if k >= 1 and k - 1 + RING < len(takes):
+            gives[k - 1].wait()
+            takes[k - 1 + RING].start()
+        if k % 2 and k // 2 < 6:
+            loads[k // 2].wait()
+            stores[k // 2].start()
+    for one in (*gives[-RING:], *puts, *stores):
+        one.wait()
+
+
 def solution(mesh):
     def step(*arrays):
         terms, weights, m, v = (arrays[i : i + 3] for i in (0, 3, 6, 9))
@@ -435,7 +468,17 @@
             name="sum_step_gather",
         )(*(pltpu.with_memory_space_constraint(one, pltpu.HBM) for one in (*(cut(t[0]) for t in terms), *wide, *m, *v)))
         whole = [one.reshape(w.shape) for one, w in zip(outs[:3], weights, strict=True)]
-        return (*whole, *outs[3:])
+        kept = [pltpu.with_memory_space_constraint(one, pltpu.HBM) for one in (whole[2], *outs[3:])]
+        dma = pltpu.SemaphoreType.DMA
+        return pl.pallas_call(
+            finish,
+            out_shape=[jax.ShapeDtypeStruct(one.shape, one.dtype) for one in (*whole[:2], *kept)],
+            in_specs=[ANY] * 9,
+            out_specs=[ANY] * 9,
+            scratch_shapes=[*(pltpu.VMEM(one.shape, one.dtype) for one in kept[1:]), pltpu.VMEM((RING, 448, 1024), jnp.bfloat16), dma((2, 8)), dma((6,)), dma((6,)), dma((RING,)), dma((RING,))],
+            compiler_params=pltpu.CompilerParams(vmem_limit_bytes=15 * 2**20),
+            name="finish",
+        )(*whole[:2], *kept)
 
     all_of, cut = P(None, None, None), P(None, "dp", None)
     return jax.shard_map(

time: 404 us -> 399 us (0.988)
  local copies, waits for them, and re-layouts: 33.5 us -> 0 us
  Pallas kernels: 370 us -> 397 us
    unnamed x23 -> x0, local copies, waits for them, and re-layouts: 33.5 us -> none
    pallas_call x0 -> x1, Pallas kernels: none -> 27.6 us  [step(): pl.pallas_call(finish, out_shape=[jax.ShapeDtypeStruct(one.shape, one.dty...]
where the time goes in v5:
time: 399 us; the launch traced here: 398 us
  Pallas kernels  397 us (99%)
    pallas_call x1, Pallas kernels, step(): pl.pallas_call(kernel, out_shape=[*((pltpu.VMEM if held else jax.ShapeDty...  370 us
    pallas_call x1, Pallas kernels, step(): pl.pallas_call(finish, out_shape=[jax.ShapeDtypeStruct(one.shape, one.dty...  27.6 us

profile of v5, /device:TPU:0, one launch (start us, length us, event | category | flops | bytes accessed | tf_op | source)
XLA Modules:
  0.0 398.1 jit_solution(17830964870917139960)
XLA Ops:
  0.6 369.8 %sum_step_gather.1 = (bf16[2,8,2,64,3584]{4,3,2,1,0:T(8,128)(2,1)S(1)}, bf16[2,8,2,64,3584]{4,3,2,1,0:T(8,128)(2,1)S(1)}, bf16[2,8,2,224,1024]{4,3,2,1,0:T(8,128...) custom-call(bf16[2,8,2,64,3584]{4,3,2,1,0:T(8,128)(2,1)} %bitcast.11, ...), custom_call_target="tpu_custom_call" | custom-call | tf_op jit(solution)/shard_map/sum_step_gather/pallas_call | solution.py:461
  370.5 27.6 %finish.1 = (bf16[2,1024,3584]{2,1,0:T(8,128)(2,1)}, bf16[2,1024,3584]{2,1,0:T(8,128)(2,1)}, bf16[2,3584,1024]{2,1,0:T(8,128)(2,1)}, f32[2,64,3584]{2,1,0:T(8,12...) custom-call(bf16[2,1024,3584]{2,1,0:T(8,128)(2,1)S(1)} %bitcast.9, ...), custom_call_target="tpu_custom_call" | custom-call | tf_op jit(solution)/shard_map/finish/pallas_call | solution.py:473

commit v6 on v5

--- a/solution.py
+++ b/solution.py
@@ -13,7 +13,7 @@
 SLOTS = 5
 INBOX = 5
 HELD = (False, False, False)
-RING = 4
+RING = 5
 LOADS = 2
 NAMES = ("gate", "up", "down")
 ALONE = 6
@@ -25,7 +25,7 @@
         return ("y",), None
     if which == 1:
         return ("y", "z"), among | (lax.rem(r + ROUNDS, 2) == 1)
-    return ("y", "z"), among & (lax.rem(r + ROUNDS, 4) == 3)
+    return ("y", "z"), among & (lax.rem(r + ROUNDS, 4) == 1)
 
 
 LAGS = {
@@ -434,7 +434,7 @@
         part, slot = (k // (3584 // rows), pl.ds(k % (3584 // rows) * rows, rows)), k % RING
         takes.append(pltpu.make_async_copy(ins[2].at[part], ring.at[slot], taken.at[slot]))
         gives.append(pltpu.make_async_copy(ring.at[slot], outs[2].at[part], given.at[slot]))
-    for one in (*takes[:RING], *loads[:2], *puts, *loads[2:]):
+    for one in (*takes[:RING], *loads, *puts):
         one.start()
     for k, (take, give) in enumerate(zip(takes, gives, strict=True)):
         take.wait()
@@ -476,7 +476,7 @@
             in_specs=[ANY] * 9,
             out_specs=[ANY] * 9,
             scratch_shapes=[*(pltpu.VMEM(one.shape, one.dtype) for one in kept[1:]), pltpu.VMEM((RING, 448, 1024), jnp.bfloat16), dma((2, 8)), dma((6,)), dma((6,)), dma((RING,)), dma((RING,))],
-            compiler_params=pltpu.CompilerParams(vmem_limit_bytes=15 * 2**20),
+            compiler_params=pltpu.CompilerParams(vmem_limit_bytes=16 * 2**20),
             name="finish",
         )(*whole[:2], *kept)
 

time: 399 us -> 398 us (level)
  no operation moved by 1% of the time
where the time goes in v6:
time: 398 us
  Pallas kernels  397 us (100%)
    pallas_call x1, Pallas kernels, step(): pl.pallas_call(kernel, out_shape=[*((pltpu.VMEM if held else jax.ShapeDty...  370 us
    pallas_call x1, Pallas kernels, step(): pl.pallas_call(finish, out_shape=[jax.ShapeDtypeStruct(one.shape, one.dty...  27.6 us

profile of v6, /device:TPU:0, one launch (start us, length us, event | category | flops | bytes accessed | tf_op | source)
XLA Modules:
  0.0 397.9 jit_solution(17068812250228849472)
XLA Ops:
  0.6 369.6 %sum_step_gather.1 = (bf16[2,8,2,64,3584]{4,3,2,1,0:T(8,128)(2,1)S(1)}, bf16[2,8,2,64,3584]{4,3,2,1,0:T(8,128)(2,1)S(1)}, bf16[2,8,2,224,1024]{4,3,2,1,0:T(8,128...) custom-call(bf16[2,8,2,64,3584]{4,3,2,1,0:T(8,128)(2,1)} %bitcast.11, ...), custom_call_target="tpu_custom_call" | custom-call | tf_op jit(solution)/shard_map/sum_step_gather/pallas_call | solution.py:461
  370.3 27.6 %finish.1 = (bf16[2,1024,3584]{2,1,0:T(8,128)(2,1)}, bf16[2,1024,3584]{2,1,0:T(8,128)(2,1)}, bf16[2,3584,1024]{2,1,0:T(8,128)(2,1)}, f32[2,64,3584]{2,1,0:T(8,12...) custom-call(bf16[2,1024,3584]{2,1,0:T(8,128)(2,1)S(1)} %bitcast.9, ...), custom_call_target="tpu_custom_call" | custom-call | tf_op jit(solution)/shard_map/finish/pallas_call | solution.py:473
